TPU v7x, 32 devices: a 4x4x1 block of a 4x4x8 slice. The times are simulated.
32 devices in a mesh: dp: 1 (over z), cp: 4 (over y), tp: 8 (over x, core).
Axes of the slice: x: 4, y: 4, z: 1, core: 2. Of those that a mesh axis runs over, the one named last changes fastest.
The devices are a block of a 4x4x8 slice.
Arguments:
- x: bfloat16 [8192, 2048], P(('dp', 'cp', 'tp'))
- idx: int32 [8192, 2], P(('dp', 'cp', 'tp'))
- gates: float32 [8192, 2], P(('dp', 'cp', 'tp'))
- wq: bfloat16 [2048, 2048], P(None, 'tp')
- wk: bfloat16 [2048, 2048], P(None, 'tp')
- wv: bfloat16 [2048, 2048], P(None, 'tp')
- wo: bfloat16 [2048, 2048], P('tp')
- w1g: bfloat16 [32, 2048, 1408], P(('cp', 'tp'))
- w1u: bfloat16 [32, 2048, 1408], P(('cp', 'tp'))
- w2: bfloat16 [32, 1408, 2048], P(('cp', 'tp'))
Outputs:
- output: bfloat16 [8192, 2048], P(('dp', 'cp', 'tp'))
All inputs are finite; a program needn't handle non-finite values.
Results may differ from a plain program's by a relative error of at most 0.0100242.
Values are sent between devices in bfloat16 or wider.
A program may use at most 768 MiB of HBM per device.

v0:
```python
import jax
import jax.numpy as jnp
from jax import lax
from jax.sharding import PartitionSpec as P

HEAD_DIM = 128
NEG = -1e30


def expert_ffn(rows, wg, wu, wd):
    gg = jnp.dot(rows, wg, preferred_element_type=jnp.float32)
    uu = jnp.dot(rows, wu, preferred_element_type=jnp.float32)
    act = (jax.nn.silu(gg) * uu).astype(jnp.bfloat16)
    return jnp.dot(act, wd, preferred_element_type=jnp.float32).astype(jnp.bfloat16)


def attention_residual(x, wq, wk, wv, wo, cp):
    rank = lax.axis_index('cp')
    xs = lax.all_gather(x, 'tp', axis=0, tiled=True)
    n = xs.shape[0]
    seg = n // 2
    q = jnp.dot(xs, wq, preferred_element_type=jnp.float32).astype(jnp.bfloat16)
    k = jnp.dot(xs, wk, preferred_element_type=jnp.float32).astype(jnp.bfloat16)
    v = jnp.dot(xs, wv, preferred_element_type=jnp.float32).astype(jnp.bfloat16)
    hq = q.shape[1] // HEAD_DIM
    hkvv = k.shape[1] // HEAD_DIM
    g = hq // hkvv
    kvs = lax.all_gather(jnp.concatenate([k, v], axis=1), 'cp', axis=0)
    rows = jnp.arange(n)

    def positions(src):
        s_id = jnp.where(rows < seg, src, 2 * cp - 1 - src)
        return s_id * seg + rows % seg

    qpos = positions(rank)
    q4 = q.reshape(n, hkvv, g, HEAD_DIM)
    scale = HEAD_DIM ** -0.5
    m = jnp.full((hkvv, g, n), NEG, jnp.float32)
    l = jnp.zeros((hkvv, g, n), jnp.float32)
    acc = jnp.zeros((hkvv, g, n, HEAD_DIM), jnp.float32)
    for j in range(cp):
        kj = kvs[j, :, :hkvv * HEAD_DIM].reshape(n, hkvv, HEAD_DIM)
        vj = kvs[j, :, hkvv * HEAD_DIM:].reshape(n, hkvv, HEAD_DIM)
        mask = positions(j)[None, :] <= qpos[:, None]
        s = jnp.einsum('nkgd,mkd->kgnm', q4, kj, preferred_element_type=jnp.float32) * scale
        s = jnp.where(mask, s, NEG)
        mn = jnp.maximum(m, jnp.max(s, axis=-1))
        w = jnp.where(mask, jnp.exp(s - mn[:, :, :, None]), 0.0)
        c = jnp.exp(m - mn)
        l = l * c + jnp.sum(w, axis=-1)
        acc = acc * c[:, :, :, None] + jnp.einsum('kgnm,mkd->kgnd', w.astype(jnp.bfloat16), vj, preferred_element_type=jnp.float32)
        m = mn
    o = (acc / l[:, :, :, None]).transpose(2, 0, 1, 3).reshape(n, hq * HEAD_DIM).astype(jnp.bfloat16)
    part = jnp.dot(o, wo, preferred_element_type=jnp.float32)
    att = lax.psum_scatter(part, 'tp', scatter_dimension=0, tiled=True)
    return (x.astype(jnp.float32) + att).astype(jnp.bfloat16)


def solution(mesh):
    cp = mesh.shape['cp']
    tp = mesh.shape['tp']
    ne = cp * tp
    rows_spec = P(('dp', 'cp', 'tp'), None)
    exp_spec = P(('cp', 'tp'), None, None)

    def local(x, idx, gates, wq, wk, wv, wo, w1g, w1u, w2):
        h = attention_residual(x, wq, wk, wv, wo, cp)
        t, hd = h.shape
        kk = idx.shape[1]
        cap = 4 * t // ne
        ea = idx.reshape(-1)
        tok = jnp.arange(t * kk) // kk
        onehot = (ea[:, None] == jnp.arange(ne)[None, :]).astype(jnp.int32)
        slot = jnp.take_along_axis(jnp.cumsum(onehot, axis=0), ea[:, None], axis=1)[:, 0] - 1
        send = jnp.zeros((ne, cap, hd), jnp.bfloat16).at[ea, slot].set(h[tok])
        recv = lax.all_to_all(send, ('cp', 'tp'), 0, 0, tiled=True)
        z = expert_ffn(recv.reshape(ne * cap, hd), w1g[0], w1u[0], w2[0])
        back = lax.all_to_all(z.reshape(ne, cap, hd), ('cp', 'tp'), 0, 0, tiled=True)
        zt = back[ea, slot].astype(jnp.float32).reshape(t, kk, hd)
        y = h.astype(jnp.float32) + jnp.sum(gates[:, :, None] * zt, axis=1)
        return y.astype(jnp.bfloat16)

    return jax.shard_map(local, mesh=mesh, in_specs=(rows_spec, rows_spec, rows_spec, P(None, 'tp'), P(None, 'tp'), P(None, 'tp'), P('tp', None), exp_spec, exp_spec, exp_spec), out_specs=rows_spec, check_vma=False)
```

profile of v0, /device:TPU:103, one launch (start us, length us, event | category | flops | bytes accessed | tf_op | source)
XLA Modules:
  0.0 777.5 jit_solution(2357145619789630392)
XLA Ops:
  6.6 0.7 all-gather.4.cloned.1.call-update
  7.3 0.1 all-gather.6.cloned.1.call-start
  7.4 49.7 %all-gather.4.cloned.1.call-done = bf16[2048,2048]{1,0:T(8,128)(2,1)} async-done(((bf16[256,2048]{1,0:T(8,128)(2,1)}), bf16[2048,2048]{1,0:T(8,128)(2,1)}) %all-gather.4.cloned.1.call-update) | async-done | bytes 8388624 | tf_op jit(solution)/shard_map/all_gather | solution.py:19
  57.1 6.1 convolution_convert_fusion.1
  63.3 0.0 copy-done.10
  63.3 0.0 copy-done.9
  63.3 2.4 convolution_convert_fusion.2
  65.7 1.5 pad_maximum_fusion
  67.2 0.1 all-gather.6.cloned.1.call-update
  67.2 0.4 reduce-scatter.2.cloned.1.call-start
  67.7 0.0 copy-start.11
  67.7 10.5 %broadcast_compare_fusion.3 = (pred[2048,2048]{0,1:T(8,128)(4,1)}, pred[2048,2048]{0,1:T(8,128)(4,1)}, pred[2048,2048]{0,1:T(8,128)(4,1)}, pred[2048,2048]{0,1:T(8,128)(4,1)}) fusion(s32[2048]{0:T(1024)S(1)} %fusion.78, s32[2048]{0:T(1024)S(1)} %fusion.79, s32[2048]{0:T(1024)S(1)} %fusion.77, s32[2048]{0:T(1024)S(1)} %fusion.76, s32[2048]{0:T(1024)S(1)} %fusion.75), kind=kLoop, calls=%fused_computation.39 | loop fusion | flops 16777216 | bytes 16818176 | tf_op jit(solution)/shard_map/le | solution.py:44
  78.2 0.0 copy-done.11
  78.2 6.7 convolution_convert_fusion
  84.9 64.7 %all-gather.6.cloned.1.call-done = bf16[8192,512]{0,1:T(8,128)(2,1)} async-done(((bf16[2048,512]{0,1:T(8,128)(2,1)}), bf16[8192,512]{0,1:T(8,128)(2,1)}) %all-gather.6.cloned.1.call-update) | async-done | bytes 8388624 | tf_op jit(solution)/shard_map/all_gather | solution.py:28
  149.6 14.6 %reshape.517 = bf16[4,2048,512]{1,0,2:T(4,128)(2,1)} reshape(bf16[8192,512]{0,1:T(8,128)(2,1)} %all-gather.6.cloned.1.call-done) | data formatting | bytes 16777216 | tf_op jit(solution)/shard_map/all_gather | solution.py:28
  164.2 24.3 %fusion.107 = (bf16[1,2048,256]{1,0,2:T(2,128)(2,1)S(1)}, bf16[1,2048,256]{1,0,2:T(2,128)(2,1)S(1)}, bf16[1,2048,256]{1,0,2:T(2,128)(2,1)S(1)}, bf16[1,2048,256]...) fusion(bf16[4,2048,512]{1,0,2:T(4,128)(2,1)} %reshape.517), kind=kLoop, calls=%fused_computation.131 | loop fusion | bytes 16777216 | tf_op jit(solution)/shard_map/slice | solution.py:43
  188.5 1.6 copy.57
  190.1 1.6 copy.63
  191.7 1.6 copy.61
  193.3 1.6 copy.59
  194.9 1.6 copy.58
  196.5 1.6 copy.60
  198.1 0.6 copy.62
  198.7 1.6 copy.64
  200.3 16.6 %fusion = (f32[2,2048]{1,0:T(2,128)S(1)}, f32[2,2048,2048]{2,1,0:T(8,128)}) fusion(pred[2048,2048]{0,1:T(8,128)(4,1)} %get-tuple-element.24, bf16[2048,2,128]{0,2,1:T(8,128)(2,1)} %bitcast.188, bf16[2048,2,128]{0,2,1:T(8,128)(2,1)} %bitcast.192), kind=kOutput, calls=%fused_computation.12 | convolution fusion | flops 2172645376 | bytes 39862272 | tf_op jit(solution)/shard_map/nkgd,mkd->kgnm/dot_general | solution.py:45
  217.0 16.1 %fusion.3 = (f32[2,2048]{1,0:T(2,128)S(1)}, f32[2,2048,2048]{2,1,0:T(8,128)}) fusion(pred[2048,2048]{0,1:T(8,128)(4,1)S(1)} %copy-done.1, bf16[2048,2,128]{0,2,1:T(8,128)(2,1)} %bitcast.187, bf16[2048,2,128]{0,2,1:T(8,128)(2,1)} %bitcast.193), kind=kOutput, calls=%fused_computation.15 | convolution fusion | flops 2172645376 | bytes 39862272 | tf_op jit(solution)/shard_map/nkgd,mkd->kgnm/dot_general | solution.py:45
  233.0 16.7 %fusion.2 = (f32[2,2048]{1,0:T(2,128)S(1)}, f32[2,2048,2048]{2,1,0:T(8,128)}) fusion(pred[2048,2048]{0,1:T(8,128)(4,1)} %get-tuple-element.26, bf16[2048,2,128]{0,2,1:T(8,128)(2,1)} %bitcast.186, bf16[2048,2,128]{0,2,1:T(8,128)(2,1)} %bitcast.194), kind=kOutput, calls=%fused_computation.14 | convolution fusion | flops 2172645376 | bytes 39862272 | tf_op jit(solution)/shard_map/nkgd,mkd->kgnm/dot_general | solution.py:45
  249.7 16.0 %fusion.1 = (f32[2,2048]{1,0:T(2,128)S(1)}, f32[2,2048,2048]{2,1,0:T(8,128)}) fusion(pred[2048,2048]{0,1:T(8,128)(4,1)S(1)} %copy-done.2, bf16[2048,2,128]{0,2,1:T(8,128)(2,1)} %bitcast.185, bf16[2048,2,128]{0,2,1:T(8,128)(2,1)} %bitcast.195), kind=kOutput, calls=%fused_computation.13 | convolution fusion | flops 2172645376 | bytes 39862272 | tf_op jit(solution)/shard_map/nkgd,mkd->kgnm/dot_general | solution.py:45
  265.7 25.6 %fusion.4 = (f32[2,2048]{1,0:T(2,128)S(1)}, f32[2,2048]{1,0:T(2,128)S(1)}) fusion(f32[2,2048,2048]{2,1,0:T(8,128)} %get-tuple-element.35, f32[2,2048]{1,0:T(2,128)S(1)} %get-tuple-element.23, pred[2048,2048]{0,1:T(8,128)(4,1)} %get-tuple-element.24, f32[2,2048]{1,0:T(2,128)S(1)} %get-tuple-element.11, f32[2,2048,2048]{2,1,0:T(8,128)} %get-tuple-element.33, ...), kind=kLoop, calls=%fused_computation.16 | loop fusion | flops 83877888 | bytes 75563008 | tf_op jit(solution)/shard_map/reduce_sum | solution.py:50
  291.4 25.4 %fusion.8 = (f32[2,2048]{1,0:T(2,128)S(1)}, f32[2,2048]{1,0:T(2,128)S(1)}) fusion(f32[2,2048,2048]{2,1,0:T(8,128)} %get-tuple-element.31, f32[2,2048]{1,0:T(2,128)S(1)} %get-tuple-element.10, pred[2048,2048]{0,1:T(8,128)(4,1)} %get-tuple-element.26, f32[2,2048]{1,0:T(2,128)S(1)} %get-tuple-element.9, f32[2,2048,2048]{2,1,0:T(8,128)} %get-tuple-element.29, ...), kind=kLoop, calls=%fused_computation.20 | loop fusion | flops 83877888 | bytes 75563008 | tf_op jit(solution)/shard_map/reduce_sum | solution.py:50
  316.8 0.1 multiply_add_fusion
  316.9 18.7 %fusion.62 = f32[2,2048,128]{1,2,0:T(8,128)} fusion(bf16[2048,2,128]{0,2,1:T(8,128)(2,1)} %bitcast.184, f32[2,2048,2048]{2,1,0:T(8,128)} %get-tuple-element.35, f32[2,2048]{1,0:T(2,128)S(1)} %get-tuple-element.23, pred[2048,2048]{0,1:T(8,128)(4,1)} %get-tuple-element.24, f32[2,2048]{1,0:T(2,128)S(1)} %get-tuple-element.6, f32[2,2048]{1,0:T(2,128)S(1)} %get-tuple-element.22), kind=kOutput, calls=%fused_computation.56 | convolution fusion | flops 2190475264 | bytes 40943616 | tf_op jit(solution)/shard_map/kgnm,mkd->kgnd/dot_general | solution.py:51
  335.5 18.9 %fusion.56 = f32[2,2048,128]{1,2,0:T(8,128)} fusion(f32[2,2048,128]{1,2,0:T(8,128)} %fusion.62, bf16[2048,2,128]{0,2,1:T(8,128)(2,1)S(1)} %bitcast.183, f32[2,2048,2048]{2,1,0:T(8,128)} %get-tuple-element.33, f32[2,2048]{1,0:T(2,128)S(1)} %get-tuple-element.11, pred[2048,2048]{0,1:T(8,128)(4,1)} %get-tuple-element.25, f32[2,2048]{1,0:T(2,128)S(1)} %get-tuple-element.7), kind=kOutput, calls=%fused_computation.54 | convolution fusion | flops 2190475264 | bytes 43024384 | tf_op jit(solution)/shard_map/kgnm,mkd->kgnd/dot_general | solution.py:51
  354.4 18.6 %fusion.50 = f32[2,2048,128]{1,2,0:T(8,128)} fusion(f32[2,2048,128]{1,2,0:T(8,128)} %fusion.56, bf16[2048,2,128]{0,2,1:T(8,128)(2,1)S(1)} %bitcast.182, f32[2,2048,2048]{2,1,0:T(8,128)} %get-tuple-element.31, f32[2,2048]{1,0:T(2,128)S(1)} %get-tuple-element.10, pred[2048,2048]{0,1:T(8,128)(4,1)} %get-tuple-element.26, f32[2,2048]{1,0:T(2,128)S(1)} %get-tuple-element.8), kind=kOutput, calls=%fused_computation.52 | convolution fusion | flops 2190475264 | bytes 43024384 | tf_op jit(solution)/shard_map/kgnm,mkd->kgnd/dot_general | solution.py:51
  373.0 17.4 %divide_convert_fusion = bf16[2,2048,128]{1,2,0:T(8,128)(2,1)S(1)} fusion(f32[2,2048]{1,0:T(2,128)S(1)} %get-tuple-element.5, f32[2,2048,128]{1,2,0:T(8,128)} %fusion.50, bf16[2048,2,128]{0,2,1:T(8,128)(2,1)S(1)} %bitcast.181, f32[2,2048,2048]{2,1,0:T(8,128)} %get-tuple-element.29, f32[2,2048]{1,0:T(2,128)S(1)} %get-tuple-element.9, ...), kind=kOutput, calls=%fused_computation.63 | convolution fusion | flops 2190999552 | bytes 41975808 | tf_op jit(solution)/shard_map/kgnm,mkd->kgnd/dot_general | solution.py:51
  390.4 0.0 copy-done
  390.4 8.1 %fusion.108 = f32[2048,2048]{1,0:T(8,128)} fusion(bf16[2048,256]{0,1:T(8,128)(2,1)S(1)} %bitcast.189, bf16[256,2048]{1,0:T(8,128)(2,1)S(1)} %copy-done), kind=kOutput, calls=%fused_computation.132 | convolution fusion | flops 2147483648 | bytes 18874368 | tf_op jit(solution)/shard_map/dot_general | solution.py:54
  398.5 0.1 reduce-scatter.2.cloned.1.call-update
  398.6 0.6 copy-done.7
  399.2 0.1 copy.41
  399.3 0.1 eq.23
  399.5 0.1 broadcast_in_dim_reshape.4
  399.6 0.1 reshape.484
  399.8 1.2 reduce-window.6
  401.0 0.2 slice_reduce_fusion
  401.3 0.1 bitcast_bitcast_fusion
  401.4 4.5 gather_fusion.2
  406.0 81.7 %reduce-scatter.2.cloned.1.call-done = f32[256,2048]{1,0:T(8,128)} async-done(((f32[2048,2048]{1,0:T(8,128)}), f32[256,2048]{1,0:T(8,128)}) %reduce-scatter.2.cloned.1.call-update) | async-done | bytes 2097168 | tf_op jit(solution)/shard_map/reduce_scatter | solution.py:55
  487.7 1.9 add_convert_fusion.1
  489.6 3.3 gather_fusion
  492.9 2.4 broadcast_in_dim.120
  495.4 92.0 %scatter_fusion = bf16[32,32,2048]{2,1,0:T(8,128)(2,1)} fusion(bf16[32,32,2048]{2,1,0:T(8,128)(2,1)} %broadcast_in_dim.120, s32[512]{0:T(512)S(1)} %bitcast.176, bf16[512,2048]{1,0:T(8,128)(2,1)} %gather_fusion), kind=kCustom, calls=%fused_computation.3 | custom fusion | bytes 6295552 | tf_op jit(solution)/shard_map/scatter | solution.py:75
  587.4 57.3 %all_to_all.10 = bf16[32,32,2048]{2,1,0:T(8,128)(2,1)S(1)} all-to-all(bf16[32,32,2048]{2,1,0:T(8,128)(2,1)} %scatter_fusion), channel_id=1, replica_groups=mesh['dp'=1,'cp'=4,'tp'=8] {'cp','tp'}, dimensions={0} | all-to-all | bytes 8388608 | tf_op jit(solution)/shard_map/all_to_all | solution.py:76
  644.7 2.1 copy-done.3
  646.8 10.2 %fusion.32 = f32[1024,1408]{1,0:T(8,128)} fusion(bf16[1024,2048]{1,0:T(8,128)(2,1)S(1)} %bitcast.179, bf16[1,2048,1408]{2,1,0:T(8,128)(2,1)} %param.17), kind=kOutput, calls=%fused_computation.44 | convolution fusion | flops 5905580032 | bytes 15728640 | tf_op jit(solution)/shard_map/dot_general | solution.py:11
  657.0 20.6 %fusion.38 = bf16[1024,2048]{1,0:T(8,128)(2,1)} fusion(bf16[1,1408,2048]{2,1,0:T(8,128)(2,1)} %param.19, f32[1024,1408]{1,0:T(8,128)} %fusion.32, bf16[1024,2048]{1,0:T(8,128)(2,1)} %bitcast.180, bf16[1,2048,1408]{2,1,0:T(8,128)(2,1)} %param.18), kind=kOutput, calls=%fused_computation.48 | convolution fusion | flops 11821907968 | bytes 25690112 | tf_op jit(solution)/shard_map/dot_general | solution.py:14
  677.7 7.9 %all-to-all-start.1 = ((bf16[32,32,2048]{2,1,0:T(8,128)(2,1)}), bf16[32,32,2048]{2,1,0:T(8,128)(2,1)}, u32[]{:S(2)}, u32[]{:S(2)}) async-start(bf16[32,32,2048]{2,1,0:T(8,128)(2,1)} %bitcast.178), calls=%async_computation.2 | async-start | bytes 8388608 | tf_op jit(solution)/shard_map/all_to_all | solution.py:78
  685.6 0.1 copy.40
  685.7 56.4 %all-to-all-done.1 = bf16[32,32,2048]{2,1,0:T(8,128)(2,1)} async-done(((bf16[32,32,2048]{2,1,0:T(8,128)(2,1)}), bf16[32,32,2048]{2,1,0:T(8,128)(2,1)}, u32[]{:S(2)}, u32[]{:S(2)}) %all-to-all-start.1) | async-done | bytes 4194336 | tf_op jit(solution)/shard_map/all_to_all | solution.py:78
  742.1 13.0 %gather_fusion.1 = bf16[512,2048]{1,0:T(8,128)(2,1)} fusion(bf16[32,32,2048]{2,1,0:T(8,128)(2,1)} %all-to-all-done.1, s32[512]{0:T(512)S(1)} %bitcast.175), kind=kCustom, calls=%fused_computation.1 | custom fusion | bytes 4198400 | tf_op jit(solution)/shard_map/gather | solution.py:79
  755.1 5.4 reshape.488
  760.5 8.9 %multiply_reduce_fusion = f32[256,2048]{1,0:T(8,128)S(1)} fusion(f32[256,2,2048]{2,1,0:T(2,128)} %reshape.488, f32[256,2]{1,0:T(8,128)S(1)} %copy.40), kind=kLoop, calls=%fused_computation.47 | loop fusion | flops 1572864 | bytes 6293504 | tf_op jit(solution)/shard_map/reduce_sum | solution.py:80
  769.4 1.3 add_convert_fusion
  (34 shorter events, 0.2 us)
Async XLA Ops:
  6.5 383.9 %copy-start = (bf16[256,2048]{1,0:T(8,128)(2,1)S(1)}, bf16[256,2048]{1,0:T(8,128)(2,1)}, u32[]{:S(2)}) copy-start(bf16[256,2048]{1,0:T(8,128)(2,1)} %param.16) | copy-start | bytes 3145732
  6.6 50.6 %all-gather.4.cloned.1.call-start = ((), (), s32[]{:S(2)}) async-start(), calls=%async_computation.3 | async-start | bytes 9437184 | tf_op jit(solution)/shard_map/all_gather | solution.py:19
  7.3 56.0 %copy-start.10 = (bf16[2048,256]{1,0:T(8,128)(2,1)S(1)}, bf16[2048,256]{1,0:T(8,128)(2,1)}, u32[]{:S(2)}) copy-start(bf16[2048,256]{1,0:T(8,128)(2,1)} %param.14) | copy-start | bytes 3145732
  7.3 142.3 %all-gather.6.cloned.1.call-start = ((), (), s32[]{:S(2)}) async-start(), calls=%async_computation.5 | async-start | bytes 10485760 | tf_op jit(solution)/shard_map/all_gather | solution.py:28
  57.1 6.2 copy-start.9
  67.2 420.5 %reduce-scatter.2.cloned.1.call-start = ((), (), s32[]{:S(2)}) async-start(), calls=%async_computation.4 | async-start | bytes 18874368 | tf_op jit(solution)/shard_map/reduce_scatter | solution.py:55
  67.7 10.5 %copy-start.11 = (bf16[2048,256]{1,0:T(8,128)(2,1)S(1)}, bf16[2048,256]{1,0:T(8,128)(2,1)}, u32[]{:S(2)}) copy-start(bf16[2048,256]{1,0:T(8,128)(2,1)} %param.13) | copy-start | bytes 3145732
  200.3 16.7 %copy-start.1 = (pred[2048,2048]{0,1:T(8,128)(4,1)S(1)}, pred[2048,2048]{0,1:T(8,128)(4,1)}, u32[]{:S(2)}) copy-start(pred[2048,2048]{0,1:T(8,128)(4,1)} %get-tuple-element.27) | copy-start | bytes 12582916
  233.0 16.7 %copy-start.2 = (pred[2048,2048]{0,1:T(8,128)(4,1)S(1)}, pred[2048,2048]{0,1:T(8,128)(4,1)}, u32[]{:S(2)}) copy-start(pred[2048,2048]{0,1:T(8,128)(4,1)} %get-tuple-element.25) | copy-start | bytes 12582916
  316.8 18.7 %copy-start.6 = (bf16[1,2048,256]{1,2,0:T(8,128)(2,1)S(1)}, bf16[1,2048,256]{1,2,0:T(8,128)(2,1)}, u32[]{:S(2)}) copy-start(bf16[1,2048,256]{1,2,0:T(8,128)(2,1)} %copy.60) | copy-start | bytes 3145732
  354.4 18.6 %copy-start.5 = (bf16[1,2048,256]{1,2,0:T(8,128)(2,1)S(1)}, bf16[1,2048,256]{1,2,0:T(8,128)(2,1)}, u32[]{:S(2)}) copy-start(bf16[1,2048,256]{1,2,0:T(8,128)(2,1)} %copy.64) | copy-start | bytes 3145732
  398.5 0.7 copy-start.7
  398.5 89.2 %copy-start.4 = (bf16[256,2048]{1,0:T(8,128)(2,1)S(1)}, bf16[256,2048]{1,0:T(8,128)(2,1)}, u32[]{:S(2)}) copy-start(bf16[256,2048]{1,0:T(8,128)(2,1)} %param.10) | copy-start | bytes 3145732
  644.7 2.1 copy-start.3
  677.7 7.9 %copy-start.8 = (f32[256,2]{0,1:T(2,128)S(1)}, f32[256,2]{0,1:T(2,128)}, u32[]{:S(2)}) copy-start(f32[256,2]{0,1:T(2,128)} %param.12) | copy-start | bytes 6148
  677.7 64.4 %all-to-all-start.1 = ((bf16[32,32,2048]{2,1,0:T(8,128)(2,1)}), bf16[32,32,2048]{2,1,0:T(8,128)(2,1)}, u32[]{:S(2)}, u32[]{:S(2)}) async-start(bf16[32,32,2048]{2,1,0:T(8,128)(2,1)} %bitcast.178), calls=%async_computation.2 | async-start | bytes 8388608 | tf_op jit(solution)/shard_map/all_to_all | solution.py:78
Sparse Core Ops, SparseCore 0:
  9.0 48.1 all-gather.3
  67.3 82.2 all-gather.5
  398.7 88.9 reduce-scatter.1
where the time goes:
time: 785 us; the launch traced here: 778 us
  waiting for transfers between devices  253 us (32%)
  matrix products  193 us (25%)
  local copies, waits for them, and re-layouts  175 us (22%)
  other arithmetic  76.6 us (10%)
  blocking collectives  57.3 us (7%)
  between operations  13.7 us (2%)
  starting transfers between devices  8.31 us (1%)
    scatter x1, local copies, waits for them, and re-layouts, local(): send = jnp.zeros((ne, cap, hd), jnp.bfloat16).at[ea, slot].set(h[tok])  92 us
    reduce_scatter x1, waiting for transfers between devices, attention_residual(): att = lax.psum_scatter(part, 'tp', scatter_dimension=0, tiled=True)  81.7 us
    dot_general x4, matrix products, attention_residual(): jnp.einsum('kgnm,mkd->kgnd', w.astype(jnp.bfloat16), vj, preferred_elemen...  73.5 us
    dot_general x4, matrix products, attention_residual(): jnp.einsum('nkgd,mkd->kgnm', q4, kj, preferred_element_type=jnp.float32)  65.4 us
    all_gather x1, waiting for transfers between devices, attention_residual(): kvs = lax.all_gather(jnp.concatenate([k, v], axis=1), 'cp', axis=0)  64.7 us
    all_to_all x1, blocking collectives, local(): recv = lax.all_to_all(send, ('cp', 'tp'), 0, 0, tiled=True)  57.3 us
    all_to_all x1, waiting for transfers between devices, local(): lax.all_to_all(z.reshape(ne, cap, hd), ('cp', 'tp'), 0, 0, tiled=True)  56.4 us
    reduce_sum x2, other arithmetic, attention_residual(): l = l * c + jnp.sum(w, axis=-1)  51 us
  transfers between devices with their start and end apart: 4, of which 4 were waited for; matrix products, arithmetic and copies ran while one was open for 3% of the time, Pallas kernels for 0%

commit v1 on v0

v1 whole, which is shorter than its diff:
```python
import functools

import jax
import jax.numpy as jnp
from jax import lax
from jax.experimental import pallas as pl
from jax.experimental.pallas import tpu as pltpu
from jax.sharding import PartitionSpec as P

HEAD_DIM = 128
NEG = -1e30
LOG2E = 1.4426950408889634
MESH = pl.DeviceIdType.MESH
HALF = 128
LAG = 3


def greet(cp, tp, c, t):
    sem = pltpu.get_barrier_semaphore()
    n = 0
    for dc in range(cp):
        for dt in range(tp):
            if dc or dt:
                peer = {'cp': lax.rem(c + dc, cp), 'tp': lax.rem(t + dt, tp)}
                pl.semaphore_signal(sem, inc=1, device_id=peer, device_id_type=MESH)
                n += 1
    pl.semaphore_wait(sem, n)


def project_kernel(cp, tp, x_ref, wq_ref, wk_ref, wv_ref, out_ref, xs, stage,
                   ss_x, ss_f, rs_x, sy, ry, sf, rf, sl):
    c = lax.axis_index('cp')
    t = lax.axis_index('tp')
    nx = tp // 2
    X = t // 2
    i = lax.rem(t, 2)
    partner = {'cp': c, 'tp': 2 * X + 1 - i}
    main = i == c // 2
    greet(cp, tp, c, t)

    def rows(hf):
        return pl.ds(pl.multiple_of(hf * HALF, HALF), HALF)

    def own_send(d, hf):
        if d == 0:
            dev, u, w = partner, 0, 1
        else:
            dev = {'cp': c, 'tp': 2 * lax.rem(X + d, nx) + i}
            u, w = {1: 2, 3: 1, 2: 3}[d], 0
        return pltpu.make_async_remote_copy(
            src_ref=x_ref.at[rows(hf)], dst_ref=xs.at[t, rows(hf)],
            send_sem=ss_x.at[d * 2 + hf], recv_sem=rs_x.at[u * 4 + w * 2 + hf],
            device_id=dev, device_id_type=MESH)

    def source(u, w):
        dx = u + (u // 2) * (5 - 2 * u)
        return 2 * lax.rem(X + dx, nx) + lax.rem(i + w, 2)

    def forward(u, hf):
        s = source(u, 0)
        return pltpu.make_async_remote_copy(
            src_ref=xs.at[s, rows(hf)], dst_ref=xs.at[s, rows(hf)],
            send_sem=ss_f.at[u * 2 + hf], recv_sem=rs_x.at[u * 4 + 2 + hf],
            device_id=partner, device_id_type=MESH)

    def landed(u, w, hf):
        s = source(u, w)
        return pltpu.make_async_remote_copy(
            src_ref=xs.at[s, rows(hf)], dst_ref=xs.at[s, rows(hf)],
            send_sem=ss_f.at[u * 2 + hf], recv_sem=rs_x.at[u * 4 + w * 2 + hf],
            device_id=partner, device_id_type=MESH)

    def place(cc, s, hf):
        seg = cc + (s // 4) * (2 * cp - 1 - 2 * cc)
        return pl.ds(pl.multiple_of(seg * 1024 + lax.rem(s, 4) * 256 + hf * HALF, HALF), HALF)

    def step_of(q):
        first = (q // 2 == 0)
        r = q - 2
        ge = r // 4
        hf = (1 - ge) * (r // 2) + ge * (r - 4)
        u = (1 - ge) * (1 + lax.rem(r, 2)) + ge * 3
        del first
        return u, hf

    def y_send(p, kk, s, hf):
        return pltpu.make_async_remote_copy(
            src_ref=stage.at[p, kk], dst_ref=out_ref.at[place(c, s, hf)],
            send_sem=sy.at[p * 2 + kk], recv_sem=ry.at[c * 16 + p],
            device_id={'cp': 2 * i + kk, 'tp': t}, device_id_type=MESH)

    def keep(p, kk, s, hf):
        return pltpu.make_async_copy(stage.at[p, kk], out_ref.at[place(c, s, hf)], sl.at[p])

    def share(p, kk, s, hf):
        return pltpu.make_async_remote_copy(
            src_ref=stage.at[p, kk], dst_ref=out_ref.at[place(c, s, hf)],
            send_sem=sf.at[c * 16 + p], recv_sem=rf.at[c * 16 + p],
            device_id=partner, device_id_type=MESH)

    def pass_on(cc, p, s, hf):
        return pltpu.make_async_remote_copy(
            src_ref=out_ref.at[place(cc, s, hf)], dst_ref=out_ref.at[place(cc, s, hf)],
            send_sem=sf.at[cc * 16 + p], recv_sem=rf.at[cc * 16 + p],
            device_id=partner, device_id_type=MESH)

    def y_landed(cc, p, s, hf):
        return pltpu.make_async_remote_copy(
            src_ref=out_ref.at[place(cc, s, hf)], dst_ref=out_ref.at[place(cc, s, hf)],
            send_sem=sf.at[cc * 16 + p], recv_sem=ry.at[cc * 16 + p],
            device_id=partner, device_id_type=MESH)

    for hf in range(2):
        for d in (1, 3, 0):
            own_send(d, hf).start()
    for hf in range(2):
        own_send(2, hf).start()

    def project(xv, p, s, hf):
        for n, w_ref in enumerate((wq_ref, wk_ref, wv_ref)):
            r = jnp.dot(xv, w_ref[...], preferred_element_type=jnp.float32).astype(jnp.bfloat16)
            for kk in range(2):
                stage[p, kk, :, n * HEAD_DIM:(n + 1) * HEAD_DIM] = r[:, kk * HEAD_DIM:(kk + 1) * HEAD_DIM]
        for kk in range(2):
            here = c == 2 * i + kk

            @pl.when(jnp.logical_not(here))
            def _():
                y_send(p, kk, s, hf).start()

            @pl.when(here)
            def _():
                keep(p, kk, s, hf).start()
                share(p, kk, s, hf).start()

    def relay(p, s, hf):
        @pl.when(main)
        def _():
            for d in range(1, cp):
                cc = lax.rem(c + d, cp)
                y_landed(cc, p, s, hf).wait_recv()
                pass_on(cc, p, s, hf).start()

    def step0(q, _):
        project(x_ref[rows(q), :], 2 * q, t, q)
        landed(0, 1, q).wait_recv()
        s = source(0, 1)
        project(xs[s, rows(q), :], 2 * q + 1, s, q)
        return 0

    lax.fori_loop(0, 2, step0, 0)

    def late(q):
        u, hf = step_of(q)
        relay(2 * q, source(u, 0), hf)
        relay(2 * q + 1, source(u, 1), hf)

    def step(q, _):
        u, hf = step_of(q)
        landed(u, 0, hf).wait_recv()
        forward(u, hf).start()
        s = source(u, 0)
        project(xs[s, rows(hf), :], 2 * q, s, hf)
        landed(u, 1, hf).wait_recv()
        s = source(u, 1)
        project(xs[s, rows(hf), :], 2 * q + 1, s, hf)

        @pl.when(q < 4)
        def _():
            relay(2 * (q - 2), t, q - 2)
            relay(2 * (q - 2) + 1, source(0, 1), q - 2)

        @pl.when(q >= 4)
        def _():
            late(q - 2)
        return 0

    lax.fori_loop(2, 8, step, 0)

    def tail(q, _):
        late(q)
        return 0

    lax.fori_loop(6, 8, tail, 0)

    for hf in range(2):
        for d in range(4):
            own_send(d, hf).wait_send()

    def drain(q, _):
        u, hf = step_of(q)
        forward(u, hf).wait_send()
        return 0

    lax.fori_loop(2, 8, drain, 0)

    def drain_pieces(p, _):
        q = p // 2
        for kk in range(2):
            here = c == 2 * i + kk

            @pl.when(jnp.logical_not(here))
            def _():
                y_send(p, kk, t, 0).wait_send()

            @pl.when(here)
            def _():
                keep(p, kk, t, 0).wait()
        del q

        @pl.when(main)
        def _():
            for cc in range(cp):
                pass_on(cc, p, t, 0).wait_send()

        @pl.when(jnp.logical_not(main))
        def _():
            for cc in range(cp):
                @pl.when(p < 4)
                def _():
                    pass_on(cc, p, lax.rem(p, 2) * (source(0, 1) - t) + t, p // 2).wait_recv()

                @pl.when(p >= 4)
                def _():
                    u, hf = step_of(p // 2)
                    pass_on(cc, p, source(u, lax.rem(p, 2)), hf).wait_recv()
        return 0

    lax.fori_loop(0, 16, drain_pieces, 0)


def project_exchange(x, wq, wk, wv, cp, tp):
    seq = x.shape[0] * cp * tp
    hd = x.shape[1]
    vm = pl.BlockSpec(memory_space=pltpu.VMEM)
    dma = pltpu.SemaphoreType.DMA
    return pl.pallas_call(
        functools.partial(project_kernel, cp, tp),
        out_shape=jax.ShapeDtypeStruct((seq, 3 * HEAD_DIM), jnp.bfloat16),
        in_specs=[vm] * 4,
        out_specs=pl.BlockSpec(memory_space=pl.ANY),
        scratch_shapes=[
            pltpu.VMEM((tp,) + x.shape, jnp.bfloat16),
            pltpu.VMEM((16, 2, HALF, 3 * HEAD_DIM), jnp.bfloat16),
            dma((8,)), dma((8,)), dma((16,)), dma((32,)), dma((64,)), dma((64,)), dma((64,)), dma((16,)),
        ],
        compiler_params=pltpu.CompilerParams(collective_id=0, has_side_effects=True, vmem_limit_bytes=48 << 20),
        name='project_exchange',
    )(x, wq, wk, wv)


QB = 256
KB = 512


def q_block(g, i):
    return 4 * (g // 2) + (1 - i) * 3 * lax.rem(g, 2) + i * (1 + lax.rem(g, 2))


def attention_kernel(qkv_ref, o_ref):
    g = pl.program_id(0)
    i = lax.rem(lax.axis_index('tp'), 2)
    b = q_block(g, i)
    q = qkv_ref[pl.ds(pl.multiple_of(b * QB, QB), QB), 0:HEAD_DIM]
    scale = HEAD_DIM ** -0.5 * LOG2E

    def chunk(off, m, l, acc, masked):
        k = qkv_ref[pl.ds(off, KB), HEAD_DIM:2 * HEAD_DIM]
        v = qkv_ref[pl.ds(off, KB), 2 * HEAD_DIM:3 * HEAD_DIM]
        s = lax.dot_general(q, k, (((1,), (1,)), ((), ())), preferred_element_type=jnp.float32) * scale
        if masked:
            qp = b * QB + lax.broadcasted_iota(jnp.int32, (QB, KB), 0)
            kp = off + lax.broadcasted_iota(jnp.int32, (QB, KB), 1)
            s = jnp.where(kp <= qp, s, NEG)
        mn = jnp.max(s, axis=1, keepdims=True)
        if m is not None:
            mn = jnp.maximum(m, mn)
        w = jnp.exp2(s - mn)
        ls = w[:, 0:128]
        for n in range(1, KB // 128):
            ls = ls + w[:, n * 128:(n + 1) * 128]
        pv = jnp.dot(w.astype(jnp.bfloat16), v, preferred_element_type=jnp.float32)
        if m is None:
            return mn, ls, pv
        c = jnp.exp2(m - mn)
        return mn, l * c + ls, acc * c + pv

    full = b // 2
    m, l, acc = chunk(pl.multiple_of(full * KB, KB), None, None, None, True)

    def body(j, carry):
        return chunk(pl.multiple_of(j * KB, KB), *carry, False)

    m, l, acc = lax.fori_loop(0, full, body, (m, l, acc))
    o_ref[0] = (acc / jnp.sum(l, axis=1, keepdims=True)).astype(jnp.bfloat16)


def attention(qkv):
    seq = qkv.shape[0]
    nb = seq // QB // 2
    return pl.pallas_call(
        attention_kernel,
        out_shape=jax.ShapeDtypeStruct((nb, QB, HEAD_DIM), jnp.bfloat16),
        grid=(nb,),
        in_specs=[pl.BlockSpec((seq, 3 * HEAD_DIM), lambda g: (0, 0))],
        out_specs=pl.BlockSpec((1, QB, HEAD_DIM), lambda g: (g, 0, 0)),
        compiler_params=pltpu.CompilerParams(vmem_limit_bytes=48 << 20),
        cost_estimate=pl.CostEstimate(flops=40_000_000_000, bytes_accessed=8 << 20, transcendentals=1 << 24),
        name='attention',
    )(qkv)


def spread_kernel(cp, tp, o_ref, out_ref, ss, rs, sl):
    c = lax.axis_index('cp')
    t = lax.axis_index('tp')
    X = t // 2
    i = lax.rem(t, 2)
    head = X * cp + c
    greet(cp, tp, c, t)
    nb = o_ref.shape[0]

    def owner(g):
        b = q_block(g, i)
        seg = b // 4
        up = seg // cp
        return seg + up * (2 * cp - 1 - 2 * seg), lax.rem(b, 4) + 4 * up

    def cols(h):
        return pl.ds(pl.multiple_of(h * HEAD_DIM, HEAD_DIM), HEAD_DIM)

    def send(g):
        oc, ot = owner(g)
        return pltpu.make_async_remote_copy(
            src_ref=o_ref.at[g], dst_ref=out_ref.at[:, cols(head)], send_sem=ss.at[g], recv_sem=rs.at[head],
            device_id={'cp': oc, 'tp': ot}, device_id_type=MESH)

    def local(g):
        return pltpu.make_async_copy(o_ref.at[g], out_ref.at[:, cols(head)], sl)

    def mine(g):
        oc, ot = owner(g)
        return jnp.logical_and(oc == c, ot == t)

    for n in range(nb):
        g = lax.rem(n * 5 + head, nb)

        @pl.when(mine(g))
        def _():
            local(g).start()

        @pl.when(jnp.logical_not(mine(g)))
        def _():
            send(g).start()

    for g in range(nb):
        @pl.when(mine(g))
        def _():
            local(g).wait()

        @pl.when(jnp.logical_not(mine(g)))
        def _():
            send(g).wait_send()
    r = lax.rem(t, 4)
    core = lax.rem((r + 1) // 2, 2)
    for h in range(nb):
        here = jnp.logical_and(h == head, core == i)

        @pl.when(jnp.logical_not(here))
        def _():
            pltpu.make_async_remote_copy(
                src_ref=o_ref.at[0], dst_ref=out_ref.at[:, cols(h)], send_sem=ss.at[0], recv_sem=rs.at[h],
                device_id={'cp': c, 'tp': 2 * X + 1 - i}, device_id_type=MESH).wait_recv()


def spread(o, cp, tp):
    nb, rows, hd = o.shape
    vm = pl.BlockSpec(memory_space=pltpu.VMEM)
    dma = pltpu.SemaphoreType.DMA
    return pl.pallas_call(
        functools.partial(spread_kernel, cp, tp),
        out_shape=jax.ShapeDtypeStruct((rows, nb * hd), jnp.bfloat16),
        in_specs=[vm],
        out_specs=vm,
        scratch_shapes=[dma((nb,)), dma((nb,)), dma],
        compiler_params=pltpu.CompilerParams(collective_id=1, has_side_effects=True),
        name='spread',
    )(o)


def expert_ffn(rows, wg, wu, wd):
    gg = jnp.dot(rows, wg, preferred_element_type=jnp.float32)
    uu = jnp.dot(rows, wu, preferred_element_type=jnp.float32)
    act = (jax.nn.silu(gg) * uu).astype(jnp.bfloat16)
    return jnp.dot(act, wd, preferred_element_type=jnp.float32).astype(jnp.bfloat16)


def routes(idx, ne, cap):
    t = idx.shape[0]
    e = jnp.arange(ne)[None, :]
    o0 = (idx[:, 0:1] == e).astype(jnp.bfloat16)
    o1 = (idx[:, 1:2] == e).astype(jnp.bfloat16)
    tri = (jnp.arange(t)[:, None] >= jnp.arange(t)[None, :]).astype(jnp.bfloat16)
    both = jnp.dot(tri, jnp.concatenate([o0, o1], axis=1), preferred_element_type=jnp.float32)
    c0 = both[:, :ne]
    c1 = both[:, ne:] + both[t - 1:, :ne]
    s0 = jnp.sum(o0.astype(jnp.float32) * c0, axis=1).astype(jnp.int32) - 1
    s1 = jnp.sum(o1.astype(jnp.float32) * c1, axis=1).astype(jnp.int32) - 1
    return idx[:, 0] * cap + s0, idx[:, 1] * cap + s1


def solution(mesh):
    cp = mesh.shape['cp']
    tp = mesh.shape['tp']
    ne = cp * tp
    rows_spec = P(('dp', 'cp', 'tp'), None)
    exp_spec = P(('cp', 'tp'), None, None)

    def local(x, idx, gates, wq, wk, wv, wo, w1g, w1u, w2):
        t, hd = x.shape
        cap = 4 * t // ne
        d0, d1 = routes(idx, ne, cap)
        qkv = project_exchange(x, wq, wk, wv, cp, tp)
        qkv, wo = lax.optimization_barrier((qkv, wo))
        wo_all = lax.all_gather(wo, 'tp', axis=0, tiled=True)
        o = spread(attention(qkv), cp, tp)
        att = jnp.dot(o, wo_all, preferred_element_type=jnp.float32)
        h = (x.astype(jnp.float32) + att).astype(jnp.bfloat16)
        places = jnp.arange(ne * cap)
        pick = jnp.logical_or(places[:, None] == d0[None, :], places[:, None] == d1[None, :]).astype(jnp.bfloat16)
        send = jnp.dot(pick, h, preferred_element_type=jnp.float32).astype(jnp.bfloat16).reshape(ne, cap, hd)
        recv = lax.all_to_all(send, ('cp', 'tp'), 0, 0, tiled=True)
        z = expert_ffn(recv.reshape(ne * cap, hd), w1g[0], w1u[0], w2[0])
        back = lax.all_to_all(z.reshape(ne, cap, hd), ('cp', 'tp'), 0, 0, tiled=True).reshape(ne * cap, hd)
        z0 = jnp.dot((d0[:, None] == places[None, :]).astype(jnp.bfloat16), back, preferred_element_type=jnp.float32)
        z1 = jnp.dot((d1[:, None] == places[None, :]).astype(jnp.bfloat16), back, preferred_element_type=jnp.float32)
        y = h.astype(jnp.float32) + gates[:, 0:1] * z0 + gates[:, 1:2] * z1
        return y.astype(jnp.bfloat16)

    return jax.shard_map(local, mesh=mesh, in_specs=(rows_spec, rows_spec, rows_spec, P(None, 'tp'), P(None, 'tp'), P(None, 'tp'), P('tp', None), exp_spec, exp_spec, exp_spec), out_specs=rows_spec, check_vma=False)
```

time: 785 us -> 346 us (0.44)
  waiting for transfers between devices: 253 us -> 56.6 us
  local copies, waits for them, and re-layouts: 175 us -> 8.2 us
  Pallas kernels: 0 us -> 157 us
  matrix products: 193 us -> 44.7 us
  other arithmetic: 76.6 us -> 0.13 us
    pallas_call x0 -> x3, Pallas kernels: none -> 157 us  [the longest x1 73.1 us: attention(): pl.pallas_call(attention_kernel, out_shape=jax.ShapeDtypeStruct((nb, QB,...]
    dot_general x12 -> x5, matrix products: 162 us -> 15.6 us  [the longest x1 6.1 us: local(): att = jnp.dot(o, wo_all, preferred_element_type=jnp.float32)]
    all_gather x2 -> x1, waiting for transfers between devices: 114 us -> 0.02 us  [local(): wo_all = lax.all_gather(wo, 'tp', axis=0, tiled=True)]
    scatter x1 -> x0, local copies, waits for them, and re-layouts: 92 us -> none  [local(): send = jnp.zeros((ne, cap, hd), jnp.bfloat16).at[ea, slot].set(h[tok])]
    reduce_scatter x1 -> x0, waiting for transfers between devices: 81.7 us -> none  [attention_residual(): att = lax.psum_scatter(part, 'tp', scatter_dimension=0, tiled=True)]
    reduce_sum x3 -> x1, other arithmetic: 59.9 us -> 0.1 us  [routes(): s0 = jnp.sum(o0.astype(jnp.float32) * c0, axis=1).astype(jnp.int32) - 1]
    slice x2 -> x3, local copies, waits for them, and re-layouts: 24.6 us -> 0.22 us  [the longest x1 0.21 us: routes(): c1 = both[:, ne:] + both[t - 1:, :ne]]
    gather x3 -> x0, local copies, waits for them, and re-layouts: 20.9 us -> none  [the longest x1 13 us: local(): zt = back[ea, slot].astype(jnp.float32).reshape(t, kk, hd)]
  transfers between devices with their start and end apart: 4 -> 2, of which waited for: 4 -> 1; matrix products, arithmetic and copies ran while one was open for 3% -> 0% of each run, Pallas kernels for 0% -> 27%
where the time goes in v1:
time: 346 us
  Pallas kernels  157 us (45%)
  blocking collectives  58.7 us (17%)
  waiting for transfers between devices  56.6 us (16%)
  matrix products  44.7 us (13%)
  between operations  13.6 us (4%)
  local copies, waits for them, and re-layouts  8.2 us (2%)
  starting transfers between devices  6.94 us (2%)
    pallas_call x1, Pallas kernels, attention(): pl.pallas_call(attention_kernel, out_shape=jax.ShapeDtypeStruct((nb, QB,...  73.1 us
    pallas_call x1, Pallas kernels, project_exchange(): pl.pallas_call(functools.partial(project_kernel, cp, tp), out_shape=jax.S...  64.6 us
    all_to_all x1, blocking collectives, local(): recv = lax.all_to_all(send, ('cp', 'tp'), 0, 0, tiled=True)  58.7 us
    all_to_all x1, waiting for transfers between devices, local(): lax.all_to_all(z.reshape(ne, cap, hd), ('cp', 'tp'), 0, 0, tiled=True)  56.6 us
    dot_general x1, matrix products, expert_ffn(): jnp.dot(act, wd, preferred_element_type=jnp.float32).astype(jnp.bfloat16)  20.6 us
    pallas_call x1, Pallas kernels, spread(): pl.pallas_call(functools.partial(spread_kernel, cp, tp), out_shape=jax.Sh...  19.4 us
    dot_general x1, matrix products, expert_ffn(): gg = jnp.dot(rows, wg, preferred_element_type=jnp.float32)  8.46 us
    unnamed x22, local copies, waits for them, and re-layouts  7.98 us
  transfers between devices with their start and end apart: 2, of which 1 were waited for; matrix products, arithmetic and copies ran while one was open for 0% of the time, Pallas kernels for 27%

profile of v1, /device:TPU:103, one launch (start us, length us, event | category | flops | bytes accessed | tf_op | source)
XLA Modules:
  0.0 346.0 jit_solution(3773145900553542181)
XLA Ops:
  6.5 0.0 all-gather.2.cloned.1.call-start
  6.6 0.0 copy-start
  6.6 1.2 copy-done
  7.8 0.0 copy-start.1
  7.8 1.2 copy-done.1
  9.0 0.0 copy-start.2
  9.0 1.2 copy-done.2
  10.2 0.0 copy-start.3
  10.2 1.2 copy-done.3
  11.5 64.6 %project_exchange.1.qkv_ref = bf16[8192,384]{1,0:T(8,128)(2,1)} custom-call(bf16[256,2048]{1,0:T(8,128)(2,1)S(1)} %copy-done.3, bf16[2048,256]{1,0:T(8,128)(2,1)S(1)} %copy-done, bf16[2048,256]{1,0:T(8,128)(2,1)S(1)} %copy-done.1, bf16[2048,256]{1,0:T(8,128)(2,1)S(1)} %copy-done.2), custom_call_target="tpu_custom_call" | custom-call | tf_op jit(solution)/shard_map/project_exchange/pallas_call | solution.py:237
  76.1 0.1 all-gather.2.cloned.1.call-update
  76.1 0.0 copy-start.7
  76.1 0.0 copy-start.4
  76.2 73.1 %attention.1.o_ref = bf16[16,256,128]{2,1,0:T(8,128)(2,1)S(1)} custom-call(bf16[8192,384]{1,0:T(8,128)(2,1)} %project_exchange.1.qkv_ref), custom_call_target="tpu_custom_call" | custom-call | flops 40000000000 | bytes 8388608 | tf_op jit(solution)/shard_map/attention/pallas_call | solution.py:301
  149.3 0.0 copy-start.5
  149.3 1.0 copy-done.5
  150.2 19.4 %spread.1 = bf16[256,2048]{1,0:T(8,128)(2,1)} custom-call(bf16[16,256,128]{2,1,0:T(8,128)(2,1)} %copy-done.5), custom_call_target="tpu_custom_call" | custom-call | tf_op jit(solution)/shard_map/spread/pallas_call | solution.py:379
  169.6 0.0 copy-done.7
  169.6 0.2 fusion.26
  169.8 0.2 slice_reduce_fusion
  170.0 0.1 fusion.29
  170.1 0.0 all-gather.2.cloned.1.call-done
  170.2 0.0 copy-done.4
  170.2 6.1 %fusion.18 = bf16[256,2048]{1,0:T(8,128)(2,1)S(1)} fusion(bf16[256,2048]{1,0:T(8,128)(2,1)} %spread.1, bf16[2048,2048]{1,0:T(8,128)(2,1)} %all-gather.2.cloned.1.call-done, bf16[256,2048]{1,0:T(8,128)(2,1)S(1)} %copy-done.4), kind=kOutput, calls=%fused_computation.15 | convolution fusion | flops 2149056512 | bytes 11534336 | tf_op jit(solution)/shard_map/dot_general | solution.py:426
  176.3 0.0 slice-start
  176.3 1.3 convolution_convert_fusion
  177.6 0.0 slice-start.1
  177.6 58.7 %all_to_all.10 = bf16[32,32,2048]{2,1,0:T(8,128)(2,1)S(1)} all-to-all(bf16[32,32,2048]{2,1,0:T(8,128)(2,1)S(1)} %bitcast.36), channel_id=1, replica_groups=mesh['dp'=1,'cp'=4,'tp'=8] {'cp','tp'}, dimensions={0} | all-to-all | bytes 8388608 | tf_op jit(solution)/shard_map/all_to_all | solution.py:431
  236.3 0.0 copy-start.6
  236.3 2.1 copy-done.6
  238.4 0.0 slice-done
  238.4 0.0 slice-done.1
  238.4 8.5 %fusion.4 = f32[1024,1408]{1,0:T(8,128)} fusion(bf16[1024,2048]{1,0:T(8,128)(2,1)S(1)} %bitcast.38, bf16[1,2048,1408]{2,1,0:T(8,128)(2,1)S(1)} %bitcast.53), kind=kOutput, calls=%fused_computation.4 | convolution fusion | flops 5905580032 | bytes 15728640 | tf_op jit(solution)/shard_map/dot_general | solution.py:391
  246.9 20.6 %fusion.10 = bf16[1024,2048]{1,0:T(8,128)(2,1)} fusion(bf16[1,1408,2048]{2,1,0:T(8,128)(2,1)} %param.19, f32[1024,1408]{1,0:T(8,128)} %fusion.4, bf16[1024,2048]{1,0:T(8,128)(2,1)} %bitcast.39, bf16[1,2048,1408]{2,1,0:T(8,128)(2,1)} %param.18), kind=kOutput, calls=%fused_computation.8 | convolution fusion | flops 11821907968 | bytes 25690112 | tf_op jit(solution)/shard_map/dot_general | solution.py:394
  267.5 0.0 copy-start.8
  267.5 6.9 %all-to-all-start.1 = ((bf16[32,32,2048]{2,1,0:T(8,128)(2,1)}), bf16[32,32,2048]{2,1,0:T(8,128)(2,1)}, u32[]{:S(2)}, u32[]{:S(2)}) async-start(bf16[32,32,2048]{2,1,0:T(8,128)(2,1)} %bitcast.37), calls=%async_computation.1 | async-start | bytes 8388608 | tf_op jit(solution)/shard_map/all_to_all | solution.py:433
  274.4 0.0 copy-done.8
  274.5 56.6 %all-to-all-done.1 = bf16[32,32,2048]{2,1,0:T(8,128)(2,1)} async-done(((bf16[32,32,2048]{2,1,0:T(8,128)(2,1)}), bf16[32,32,2048]{2,1,0:T(8,128)(2,1)}, u32[]{:S(2)}, u32[]{:S(2)}) %all-to-all-start.1) | async-done | bytes 4194336 | tf_op jit(solution)/shard_map/all_to_all | solution.py:433
  331.1 3.5 %convolution_multiply_fusion = f32[256,2048]{1,0:T(8,128)S(1)} fusion(bf16[1024,2048]{1,0:T(8,128)(2,1)} %bitcast.11, f32[256]{0:T(256)S(1)} %bitcast.50, s32[256]{0:T(256)S(1)} %bitcast.51), kind=kOutput, calls=%fused_computation.10 | convolution fusion | flops 1074528256 | bytes 6293504 | tf_op jit(solution)/shard_map/dot_general | solution.py:435
  334.6 4.6 %fusion.19 = bf16[256,2048]{1,0:T(8,128)(2,1)} fusion(f32[256,2048]{1,0:T(8,128)S(1)} %convolution_multiply_fusion, bf16[1024,2048]{1,0:T(8,128)(2,1)} %bitcast.11, bf16[256,2048]{1,0:T(8,128)(2,1)S(1)} %fusion.18, f32[256]{0:T(256)S(1)} %bitcast.48, s32[256]{0:T(256)S(1)} %bitcast.49), kind=kOutput, calls=%fused_computation.16 | convolution fusion | flops 1076625408 | bytes 8390656 | tf_op jit(solution)/shard_map/dot_general | solution.py:434
  (7 shorter events, 0.0 us)
Async XLA Ops:
  6.5 163.6 %all-gather.2.cloned.1.call-start = ((), (), s32[]{:S(2)}) async-start(), calls=%async_computation.2 | async-start | bytes 9437184 | tf_op jit(solution)/shard_map/all_gather | solution.py:424
  6.6 1.2 copy-start
  7.8 1.2 copy-start.1
  9.0 1.2 copy-start.2
  10.2 1.2 copy-start.3
  76.1 93.5 %copy-start.7 = (s32[256,2]{0,1:T(2,128)S(1)}, s32[256,2]{0,1:T(2,128)}, u32[]{:S(2)}) copy-start(s32[256,2]{0,1:T(2,128)} %param.11) | copy-start | bytes 6148
  76.1 94.0 %copy-start.4 = (bf16[256,2048]{1,0:T(8,128)(2,1)S(1)}, bf16[256,2048]{1,0:T(8,128)(2,1)}, u32[]{:S(2)}) copy-start(bf16[256,2048]{1,0:T(8,128)(2,1)} %x_ref.1) | copy-start | bytes 3145732
  149.3 1.0 copy-start.5
  176.3 62.1 %slice-start = ((s8[5767168]{0:T(1024)(128)(4,1)}), s8[4194304]{0:T(1024)(128)(4,1)S(1)}, s32[]{:S(2)}) async-start(s8[5767168]{0:T(1024)(128)(4,1)} %bitcast.52), calls=%async_computation.3 | async-start | bytes 8388608
  177.6 60.8 %slice-start.1 = ((s8[5767168]{0:T(1024)(128)(4,1)}), s8[1572864]{0:T(1024)(128)(4,1)S(1)}, s32[]{:S(2)}) async-start(s8[5767168]{0:T(1024)(128)(4,1)} %bitcast.52), calls=%async_computation.4 | async-start | bytes 3145728
  236.3 2.1 copy-start.6
  267.5 7.0 %copy-start.8 = (f32[256,2]{0,1:T(2,128)S(1)}, f32[256,2]{0,1:T(2,128)}, u32[]{:S(2)}) copy-start(f32[256,2]{0,1:T(2,128)} %param.12) | copy-start | bytes 6148
  267.5 63.6 %all-to-all-start.1 = ((bf16[32,32,2048]{2,1,0:T(8,128)(2,1)}), bf16[32,32,2048]{2,1,0:T(8,128)(2,1)}, u32[]{:S(2)}, u32[]{:S(2)}) async-start(bf16[32,32,2048]{2,1,0:T(8,128)(2,1)} %bitcast.37), calls=%async_computation.1 | async-start | bytes 8388608 | tf_op jit(solution)/shard_map/all_to_all | solution.py:433
Sparse Core Ops, SparseCore 0:
  76.3 44.8 all-gather.1

commit v2 on v1

--- a/solution.py
+++ b/solution.py
@@ -250,7 +250,7 @@
 
 
 QB = 256
-KB = 512
+KB = 1024
 
 
 def q_block(g, i):
@@ -258,21 +258,26 @@
 
 
 def attention_kernel(qkv_ref, o_ref):
-    g = pl.program_id(0)
+    seg = pl.program_id(0)
     i = lax.rem(lax.axis_index('tp'), 2)
-    b = q_block(g, i)
-    q = qkv_ref[pl.ds(pl.multiple_of(b * QB, QB), QB), 0:HEAD_DIM]
+    blocks = [q_block(2 * seg + n, i) for n in range(2)]
+    q = jnp.concatenate([qkv_ref[pl.ds(pl.multiple_of(b * QB, QB), QB), 0:HEAD_DIM] for b in blocks], axis=0)
     scale = HEAD_DIM ** -0.5 * LOG2E
 
-    def chunk(off, m, l, acc, masked):
+    def chunk(j, m, l, acc, masked):
+        off = pl.multiple_of(j * KB, KB)
         k = qkv_ref[pl.ds(off, KB), HEAD_DIM:2 * HEAD_DIM]
         v = qkv_ref[pl.ds(off, KB), 2 * HEAD_DIM:3 * HEAD_DIM]
         s = lax.dot_general(q, k, (((1,), (1,)), ((), ())), preferred_element_type=jnp.float32) * scale
         if masked:
-            qp = b * QB + lax.broadcasted_iota(jnp.int32, (QB, KB), 0)
-            kp = off + lax.broadcasted_iota(jnp.int32, (QB, KB), 1)
+            row = lax.broadcasted_iota(jnp.int32, (2 * QB, KB), 0)
+            qp = jnp.where(row < QB, blocks[0] * QB + row, (blocks[1] - 1) * QB + row)
+            kp = off + lax.broadcasted_iota(jnp.int32, (2 * QB, KB), 1)
             s = jnp.where(kp <= qp, s, NEG)
-        mn = jnp.max(s, axis=1, keepdims=True)
+        mn = s[:, 0:128]
+        for n in range(1, KB // 128):
+            mn = jnp.maximum(mn, s[:, n * 128:(n + 1) * 128])
+        mn = jnp.max(mn, axis=1, keepdims=True)
         if m is not None:
             mn = jnp.maximum(m, mn)
         w = jnp.exp2(s - mn)
@@ -285,14 +290,11 @@
         c = jnp.exp2(m - mn)
         return mn, l * c + ls, acc * c + pv
 
-    full = b // 2
-    m, l, acc = chunk(pl.multiple_of(full * KB, KB), None, None, None, True)
-
-    def body(j, carry):
-        return chunk(pl.multiple_of(j * KB, KB), *carry, False)
-
-    m, l, acc = lax.fori_loop(0, full, body, (m, l, acc))
-    o_ref[0] = (acc / jnp.sum(l, axis=1, keepdims=True)).astype(jnp.bfloat16)
+    first = chunk(seg, None, None, None, True)
+    m, l, acc = lax.fori_loop(0, seg, lambda j, carry: chunk(j, *carry, False), first)
+    o = (acc / jnp.sum(l, axis=1, keepdims=True)).astype(jnp.bfloat16)
+    o_ref[0] = o[:QB]
+    o_ref[1] = o[QB:]
 
 
 def attention(qkv):
@@ -301,9 +303,9 @@
     return pl.pallas_call(
         attention_kernel,
         out_shape=jax.ShapeDtypeStruct((nb, QB, HEAD_DIM), jnp.bfloat16),
-        grid=(nb,),
+        grid=(nb // 2,),
         in_specs=[pl.BlockSpec((seq, 3 * HEAD_DIM), lambda g: (0, 0))],
-        out_specs=pl.BlockSpec((1, QB, HEAD_DIM), lambda g: (g, 0, 0)),
+        out_specs=pl.BlockSpec((2, QB, HEAD_DIM), lambda g: (g, 0, 0)),
         compiler_params=pltpu.CompilerParams(vmem_limit_bytes=48 << 20),
         cost_estimate=pl.CostEstimate(flops=40_000_000_000, bytes_accessed=8 << 20, transcendentals=1 << 24),
         name='attention',
@@ -387,11 +389,105 @@
     )(o)
 
 
-def expert_ffn(rows, wg, wu, wd):
-    gg = jnp.dot(rows, wg, preferred_element_type=jnp.float32)
-    uu = jnp.dot(rows, wu, preferred_element_type=jnp.float32)
-    act = (jax.nn.silu(gg) * uu).astype(jnp.bfloat16)
-    return jnp.dot(act, wd, preferred_element_type=jnp.float32).astype(jnp.bfloat16)
+CHIPS = ((2, 2), (1, 0), (0, 1), (3, 0), (0, 3), (1, 1), (3, 3), (1, 3), (3, 1), (2, 0), (0, 2), (2, 1), (1, 2), (2, 3), (3, 2), (0, 0))
+GROUP = 4
+
+
+def experts_kernel(cp, tp, send_ref, wg_hbm, wu_hbm, wd_hbm, back_ref, recv, z, wg, wu, wd,
+                   ss, rs, sb, rb, sw, sl):
+    c = lax.axis_index('cp')
+    t = lax.axis_index('tp')
+    nx = tp // 2
+    X = t // 2
+    i = lax.rem(t, 2)
+    me = c * tp + t
+    n_dev = cp * tp
+    offs = [(a, b, k) for a, b in CHIPS for k in range(2) if (a, b, k) != (0, 0, 0)]
+    weights = [pltpu.make_async_copy(h, v, sw.at[n]) for n, (h, v) in enumerate(((wg_hbm, wg), (wu_hbm, wu), (wd_hbm, wd)))]
+    for w in weights:
+        w.start()
+    greet(cp, tp, c, t)
+
+    def target(o):
+        s = 1 - 2 * i
+        return lax.rem(c + s * o[0] + cp, cp), 2 * lax.rem(X + s * o[1] + nx, nx) + lax.rem(i + o[2], 2)
+
+    def origin(o):
+        j = lax.rem(i + o[2], 2)
+        s = 1 - 2 * j
+        return lax.rem(c - s * o[0] + cp, cp), 2 * lax.rem(X - s * o[1] + nx, nx) + j
+
+    def out(k):
+        pc, pt = target(offs[k])
+        return pltpu.make_async_remote_copy(
+            src_ref=send_ref.at[pc * tp + pt], dst_ref=recv.at[k], send_sem=ss.at[k], recv_sem=rs.at[k],
+            device_id={'cp': pc, 'tp': pt}, device_id_type=MESH)
+
+    def home(k):
+        pc, pt = origin(offs[k])
+        return pltpu.make_async_remote_copy(
+            src_ref=z.at[k], dst_ref=back_ref.at[me], send_sem=sb.at[k], recv_sem=rb.at[k],
+            device_id={'cp': pc, 'tp': pt}, device_id_type=MESH)
+
+    last = n_dev - 1
+    for k in range(last):
+        out(k).start()
+    own = pltpu.make_async_copy(send_ref.at[me], recv.at[last], sl.at[0])
+    own.start()
+    for w in weights:
+        w.wait()
+    cap, hd = recv.shape[1:]
+
+    def group(n, _):
+        for k in range(last):
+            @pl.when(n == k // GROUP)
+            def _():
+                out(k).wait_recv()
+
+        @pl.when(n == last // GROUP)
+        def _():
+            own.wait()
+
+        rows = recv[pl.ds(n * GROUP, GROUP)].reshape(GROUP * cap, hd)
+        gg = jnp.dot(rows, wg[...], preferred_element_type=jnp.float32)
+        uu = jnp.dot(rows, wu[...], preferred_element_type=jnp.float32)
+        act = (gg * jax.nn.sigmoid(gg) * uu).astype(jnp.bfloat16)
+        r = jnp.dot(act, wd[...], preferred_element_type=jnp.float32).astype(jnp.bfloat16)
+        z[pl.ds(n * GROUP, GROUP)] = r.reshape(GROUP, cap, hd)
+        for k in range(last):
+            @pl.when(n == k // GROUP)
+            def _():
+                home(k).start()
+        return 0
+
+    lax.fori_loop(0, n_dev // GROUP, group, 0)
+    keep = pltpu.make_async_copy(z.at[last], back_ref.at[me], sl.at[1])
+    keep.start()
+    for k in range(last):
+        out(k).wait_send()
+    for k in range(last):
+        home(k).wait_send()
+        home(k).wait_recv()
+    keep.wait()
+
+
+def experts(send, wg, wu, wd, cp, tp):
+    anym = pl.BlockSpec(memory_space=pl.ANY)
+    dma = pltpu.SemaphoreType.DMA
+    n = send.shape[0]
+    return pl.pallas_call(
+        functools.partial(experts_kernel, cp, tp),
+        out_shape=jax.ShapeDtypeStruct(send.shape, jnp.bfloat16),
+        in_specs=[pl.BlockSpec(memory_space=pltpu.VMEM), anym, anym, anym],
+        out_specs=pl.BlockSpec(memory_space=pltpu.VMEM),
+        scratch_shapes=[
+            pltpu.VMEM(send.shape, jnp.bfloat16), pltpu.VMEM(send.shape, jnp.bfloat16),
+            pltpu.VMEM(wg.shape, jnp.bfloat16), pltpu.VMEM(wu.shape, jnp.bfloat16), pltpu.VMEM(wd.shape, jnp.bfloat16),
+            dma((n,)), dma((n,)), dma((n,)), dma((n,)), dma((3,)), dma((2,)),
+        ],
+        compiler_params=pltpu.CompilerParams(collective_id=2, has_side_effects=True, vmem_limit_bytes=60 << 20),
+        name='experts',
+    )(send, wg, wu, wd)
 
 
 def routes(idx, ne, cap):
@@ -428,9 +524,7 @@
         places = jnp.arange(ne * cap)
         pick = jnp.logical_or(places[:, None] == d0[None, :], places[:, None] == d1[None, :]).astype(jnp.bfloat16)
         send = jnp.dot(pick, h, preferred_element_type=jnp.float32).astype(jnp.bfloat16).reshape(ne, cap, hd)
-        recv = lax.all_to_all(send, ('cp', 'tp'), 0, 0, tiled=True)
-        z = expert_ffn(recv.reshape(ne * cap, hd), w1g[0], w1u[0], w2[0])
-        back = lax.all_to_all(z.reshape(ne, cap, hd), ('cp', 'tp'), 0, 0, tiled=True).reshape(ne * cap, hd)
+        back = experts(send, w1g[0], w1u[0], w2[0], cp, tp).reshape(ne * cap, hd)
         z0 = jnp.dot((d0[:, None] == places[None, :]).astype(jnp.bfloat16), back, preferred_element_type=jnp.float32)
         z1 = jnp.dot((d1[:, None] == places[None, :]).astype(jnp.bfloat16), back, preferred_element_type=jnp.float32)
         y = h.astype(jnp.float32) + gates[:, 0:1] * z0 + gates[:, 1:2] * z1

time: 346 us -> 281 us (0.81); the launches traced: 346 us -> 277 us
  Pallas kernels: 157 us -> 242 us
  blocking collectives: 58.7 us -> 0 us
  waiting for transfers between devices: 56.6 us -> 0.08 us
  matrix products: 44.7 us -> 15.6 us
  starting transfers between devices: 6.94 us -> 0.01 us
    pallas_call x0 -> x1, Pallas kernels: none -> 113 us  [experts(): pl.pallas_call(functools.partial(experts_kernel, cp, tp), out_shape=jax.S...]
    all_to_all x1 -> x0, blocking collectives: 58.7 us -> none  [local(): recv = lax.all_to_all(send, ('cp', 'tp'), 0, 0, tiled=True)]
    all_to_all x1 -> x0, waiting for transfers between devices: 56.6 us -> none  [local(): lax.all_to_all(z.reshape(ne, cap, hd), ('cp', 'tp'), 0, 0, tiled=True)]
    dot_general x2 -> x0, matrix products: 29.1 us -> none  [the longest x1 20.6 us: expert_ffn(): jnp.dot(act, wd, preferred_element_type=jnp.float32).astype(jnp.bfloat16)]
    pallas_call x1, Pallas kernels: 73.1 us -> 44.8 us  [attention(): pl.pallas_call(attention_kernel, out_shape=jax.ShapeDtypeStruct((nb, QB,...]
    all_to_all x1 -> x0, starting transfers between devices: 6.94 us -> none  [local(): lax.all_to_all(z.reshape(ne, cap, hd), ('cp', 'tp'), 0, 0, tiled=True)]
    unnamed x22 -> x18, local copies, waits for them, and re-layouts: 7.98 us -> 5.89 us
  transfers between devices with their start and end apart: 2 -> 1, of which waited for: 1 -> 0; matrix products, arithmetic and copies ran while one was open for 0% -> 0% of each run, Pallas kernels for 27% -> 23%
where the time goes in v2:
time: 281 us; the launch traced here: 277 us
  Pallas kernels  242 us (86%)
  matrix products  15.6 us (6%)
  between operations  13.6 us (5%)
  local copies, waits for them, and re-layouts  6.1 us (2%)
    pallas_call x1, Pallas kernels, experts(): pl.pallas_call(functools.partial(experts_kernel, cp, tp), out_shape=jax.S...  113 us
    pallas_call x1, Pallas kernels, project_exchange(): pl.pallas_call(functools.partial(project_kernel, cp, tp), out_shape=jax.S...  64.6 us
    pallas_call x1, Pallas kernels, attention(): pl.pallas_call(attention_kernel, out_shape=jax.ShapeDtypeStruct((nb, QB,...  44.8 us
    pallas_call x1, Pallas kernels, spread(): pl.pallas_call(functools.partial(spread_kernel, cp, tp), out_shape=jax.Sh...  19.4 us
    dot_general x1, matrix products, local(): att = jnp.dot(o, wo_all, preferred_element_type=jnp.float32)  6.07 us
    unnamed x18, local copies, waits for them, and re-layouts  5.89 us
  transfers between devices with their start and end apart: 1, of which 0 were waited for; matrix products, arithmetic and copies ran while one was open for 0% of the time, Pallas kernels for 23%

profile of v2, /device:TPU:103, one launch (start us, length us, event | category | flops | bytes accessed | tf_op | source)
XLA Modules:
  0.0 277.2 jit_solution(10103256727245753187)
XLA Ops:
  6.5 0.0 all-gather.2.cloned.1.call-start
  6.6 0.0 copy-start
  6.6 1.2 copy-done
  7.8 0.0 copy-start.1
  7.8 1.2 copy-done.1
  9.0 0.0 copy-start.2
  9.0 1.2 copy-done.2
  10.2 0.0 copy-start.3
  10.2 1.2 copy-done.3
  11.5 64.6 %project_exchange.1.qkv_ref = bf16[8192,384]{1,0:T(8,128)(2,1)} custom-call(bf16[256,2048]{1,0:T(8,128)(2,1)S(1)} %copy-done.3, bf16[2048,256]{1,0:T(8,128)(2,1)S(1)} %copy-done, bf16[2048,256]{1,0:T(8,128)(2,1)S(1)} %copy-done.1, bf16[2048,256]{1,0:T(8,128)(2,1)S(1)} %copy-done.2), custom_call_target="tpu_custom_call" | custom-call | tf_op jit(solution)/shard_map/project_exchange/pallas_call | solution.py:237
  76.1 0.1 all-gather.2.cloned.1.call-update
  76.1 0.0 copy-start.7
  76.1 0.0 copy-start.8
  76.2 0.0 copy-start.4
  76.2 44.8 %attention.1.o_ref = bf16[16,256,128]{2,1,0:T(8,128)(2,1)S(1)} custom-call(bf16[8192,384]{1,0:T(8,128)(2,1)} %project_exchange.1.qkv_ref), custom_call_target="tpu_custom_call" | custom-call | flops 40000000000 | bytes 8388608 | tf_op jit(solution)/shard_map/attention/pallas_call | solution.py:303
  120.9 0.0 copy-start.5
  121.0 1.0 copy-done.5
  121.9 19.4 %spread.1 = bf16[256,2048]{1,0:T(8,128)(2,1)} custom-call(bf16[16,256,128]{2,1,0:T(8,128)(2,1)} %copy-done.5), custom_call_target="tpu_custom_call" | custom-call | tf_op jit(solution)/shard_map/spread/pallas_call | solution.py:381
  141.3 0.0 copy-done.7
  141.3 0.2 fusion.10
  141.5 0.2 slice_reduce_fusion
  141.7 0.1 fusion.13
  141.8 0.0 copy-done.8
  141.9 0.0 all-gather.2.cloned.1.call-done
  141.9 0.0 copy-done.4
  141.9 6.1 %fusion.2 = bf16[256,2048]{1,0:T(8,128)(2,1)S(1)} fusion(bf16[256,2048]{1,0:T(8,128)(2,1)} %spread.1, bf16[2048,2048]{1,0:T(8,128)(2,1)} %all-gather.2.cloned.1.call-done, bf16[256,2048]{1,0:T(8,128)(2,1)S(1)} %copy-done.4), kind=kOutput, calls=%fused_computation.6 | convolution fusion | flops 2149056512 | bytes 11534336 | tf_op jit(solution)/shard_map/dot_general | solution.py:522
  148.0 3.2 %convolution_convert_fusion = bf16[1024,2048]{1,0:T(8,128)(2,1)} fusion(bf16[256,2048]{1,0:T(8,128)(2,1)S(1)} %fusion.2, s32[256]{0:T(256)S(1)} %get-tuple-element.20, s32[256]{0:T(256)S(1)} %get-tuple-element.18), kind=kOutput, calls=%fused_computation | convolution fusion | flops 1076625408 | bytes 5244928 | tf_op jit(solution)/shard_map/dot_general | solution.py:526
  151.2 113.0 %experts.1 = bf16[32,32,2048]{2,1,0:T(8,128)(2,1)} custom-call(bf16[32,32,2048]{2,1,0:T(8,128)(2,1)} %bitcast.18, bf16[2048,1408]{1,0:T(8,128)(2,1)} %bitcast.19, bf16[2048,1408]{1,0:T(8,128)(2,1)} %bitcast.20, bf16[1408,2048]{1,0:T(8,128)(2,1)} %bitcast.21), custom_call_target="tpu_custom_call" | custom-call | tf_op jit(solution)/shard_map/experts/pallas_call | solution.py:478
  264.2 0.0 copy-start.6
  264.2 3.6 %convolution_multiply_fusion = f32[256,2048]{1,0:T(8,128)S(1)} fusion(bf16[1024,2048]{1,0:T(8,128)(2,1)} %bitcast.22, f32[256]{0:T(256)S(1)} %bitcast.34, s32[256]{0:T(256)S(1)} %bitcast.35), kind=kOutput, calls=%fused_computation.1 | convolution fusion | flops 1074528256 | bytes 6293504 | tf_op jit(solution)/shard_map/dot_general | solution.py:529
  267.8 0.0 copy-done.6
  267.8 2.5 fusion.3
  (6 shorter events, 0.0 us)
Async XLA Ops:
  6.5 135.3 %all-gather.2.cloned.1.call-start = ((), (), s32[]{:S(2)}) async-start(), calls=%async_computation | async-start | bytes 9437184 | tf_op jit(solution)/shard_map/all_gather | solution.py:520
  6.6 1.2 copy-start
  7.8 1.2 copy-start.1
  9.0 1.2 copy-start.2
  10.2 1.2 copy-start.3
  76.1 65.2 %copy-start.7 = (s32[256,2]{0,1:T(2,128)S(1)}, s32[256,2]{0,1:T(2,128)}, u32[]{:S(2)}) copy-start(s32[256,2]{0,1:T(2,128)} %param.11) | copy-start | bytes 6148
  76.1 65.7 %copy-start.8 = (f32[256,2]{0,1:T(2,128)S(1)}, f32[256,2]{0,1:T(2,128)}, u32[]{:S(2)}) copy-start(f32[256,2]{0,1:T(2,128)} %param.12) | copy-start | bytes 6148
  76.2 65.7 %copy-start.4 = (bf16[256,2048]{1,0:T(8,128)(2,1)S(1)}, bf16[256,2048]{1,0:T(8,128)(2,1)}, u32[]{:S(2)}) copy-start(bf16[256,2048]{1,0:T(8,128)(2,1)} %x_ref.1) | copy-start | bytes 3145732
  120.9 1.0 copy-start.5
  264.2 3.7 %copy-start.6 = (bf16[32,32,2048]{2,1,0:T(8,128)(2,1)S(1)}, bf16[32,32,2048]{2,1,0:T(8,128)(2,1)}, u32[]{:S(2)}) copy-start(bf16[32,32,2048]{2,1,0:T(8,128)(2,1)} %experts.1) | copy-start | bytes 12582916
Sparse Core Ops, SparseCore 0:
  76.3 44.8 all-gather.1

commit v3 on v2

v3 whole, which is shorter than its diff:
```python
import functools

import jax
import jax.numpy as jnp
from jax import lax
from jax.experimental import pallas as pl
from jax.experimental.pallas import tpu as pltpu
from jax.sharding import PartitionSpec as P

HEAD_DIM = 128
NEG = -1e30
LOG2E = 1.4426950408889634
MESH = pl.DeviceIdType.MESH
HALF = 128
LAG = 4


def greet(cp, tp, c, t):
    sem = pltpu.get_barrier_semaphore()
    n = 0
    for dc in range(cp):
        for dt in range(tp):
            if dc or dt:
                peer = {'cp': lax.rem(c + dc, cp), 'tp': lax.rem(t + dt, tp)}
                pl.semaphore_signal(sem, inc=1, device_id=peer, device_id_type=MESH)
                n += 1
    pl.semaphore_wait(sem, n)


class Gather:
    def __init__(self, cp, tp, c, t, src, dst, send, passed, recv):
        self.c, self.t, self.nx = c, t, tp // 2
        self.X, self.i = t // 2, lax.rem(t, 2)
        self.partner = {'cp': c, 'tp': 2 * self.X + 1 - self.i}
        self.src, self.dst, self.send, self.passed, self.recv = src, dst, send, passed, recv

    def chip(self, d):
        return {'cp': self.c, 'tp': 2 * lax.rem(self.X + d, self.nx) + self.i}

    def source(self, u, w):
        dx = u + (u // 2) * (5 - 2 * u)
        return 2 * lax.rem(self.X + dx, self.nx) + lax.rem(self.i + w, 2)

    def copy(self, src, dst, send, u, w, hf, dev):
        return pltpu.make_async_remote_copy(
            src_ref=src, dst_ref=dst, send_sem=send, recv_sem=self.recv.at[u * 4 + w * 2 + hf],
            device_id=dev, device_id_type=MESH)

    def own(self, d, hf):
        dev, u, w = {0: (self.partner, 0, 1), 1: (self.chip(1), 2, 0), 3: (self.chip(3), 1, 0)}[d]
        return self.copy(self.src(hf), self.dst(self.t, hf), self.send.at[d * 2 + hf], u, w, hf, dev)

    def relay(self, hf):
        ref = self.dst(self.source(2 - hf, 0), hf)
        return self.copy(ref, ref, self.send.at[4 + hf], 3, 0, hf, self.chip(1 + 2 * hf))

    def share(self, u, hf):
        ref = self.dst(self.source(u, 0), hf)
        return self.copy(ref, ref, self.passed.at[u * 2 + hf], u, 1, hf, self.partner)

    def landed(self, u, w, hf):
        ref = self.dst(self.source(u, w), hf)
        return self.copy(ref, ref, self.passed.at[0], u, w, hf, self.partner)

    def start(self):
        for first in range(2):
            self.own(1, first).start()
            self.own(3, 1 - first).start()
            self.own(0, first).start()

    def drain(self):
        for hf in range(2):
            for d in (0, 1, 3):
                self.own(d, hf).wait_send()
            self.relay(hf).wait_send()
            for u in range(1, 4):
                self.share(u, hf).wait_send()


def project_kernel(cp, tp, x_hbm, wq_hbm, wk_hbm, wv_hbm, out_ref, xs, stage, wq_ref, wk_ref, wv_ref,
                   ss_x, ss_f, rs_x, sy, ry, sf, rf, sl, sw):
    c = lax.axis_index('cp')
    t = lax.axis_index('tp')
    X = t // 2
    i = lax.rem(t, 2)
    partner = {'cp': c, 'tp': 2 * X + 1 - i}
    main = i == c // 2
    loads = [pltpu.make_async_copy(h, v, sw.at[n]) for n, (h, v) in enumerate(
        ((x_hbm, xs.at[t]), (wq_hbm, wq_ref), (wk_hbm, wk_ref), (wv_hbm, wv_ref)))]
    for load in loads:
        load.start()
    greet(cp, tp, c, t)

    def rows(hf):
        return pl.ds(pl.multiple_of(hf * HALF, HALF), HALF)

    gather = Gather(cp, tp, c, t, lambda hf: x_hbm.at[rows(hf)], lambda s, hf: xs.at[s, rows(hf)], ss_x, ss_f, rs_x)
    source = gather.source

    def place(cc, s, hf):
        seg = cc + (s // 4) * (2 * cp - 1 - 2 * cc)
        return pl.ds(pl.multiple_of(seg * 1024 + lax.rem(s, 4) * 256 + hf * HALF, HALF), HALF)

    def piece(p):
        stage = p // 4
        w, v = lax.rem(p, 4) // 2, lax.rem(p, 2)
        first, last = (3 - stage) // 3, stage // 3
        mid = 1 - first - last
        return mid * (1 + v) + 3 * last, w, (1 - mid) * v + mid * lax.rem(stage + v, 2)

    def whose(p):
        u, w, hf = piece(p)
        return source(u, w), hf

    def y_send(p, kk, s, hf):
        return pltpu.make_async_remote_copy(
            src_ref=stage.at[p, kk], dst_ref=out_ref.at[place(c, s, hf)],
            send_sem=sy.at[p * 2 + kk], recv_sem=ry.at[c * 16 + p],
            device_id={'cp': 2 * i + kk, 'tp': t}, device_id_type=MESH)

    def keep(p, kk, s, hf):
        return pltpu.make_async_copy(stage.at[p, kk], out_ref.at[place(c, s, hf)], sl.at[p])

    def share(p, kk, s, hf):
        return pltpu.make_async_remote_copy(
            src_ref=stage.at[p, kk], dst_ref=out_ref.at[place(c, s, hf)],
            send_sem=sf.at[c * 16 + p], recv_sem=rf.at[c * 16 + p],
            device_id=partner, device_id_type=MESH)

    def pass_on(cc, p, s, hf):
        return pltpu.make_async_remote_copy(
            src_ref=out_ref.at[place(cc, s, hf)], dst_ref=out_ref.at[place(cc, s, hf)],
            send_sem=sf.at[cc * 16 + p], recv_sem=rf.at[cc * 16 + p],
            device_id=partner, device_id_type=MESH)

    def y_landed(cc, p, s, hf):
        return pltpu.make_async_remote_copy(
            src_ref=out_ref.at[place(cc, s, hf)], dst_ref=out_ref.at[place(cc, s, hf)],
            send_sem=sf.at[cc * 16 + p], recv_sem=ry.at[cc * 16 + p],
            device_id=partner, device_id_type=MESH)

    gather.start()
    for load in loads:
        load.wait()

    def project(xv, p, s, hf):
        for n, w_ref in enumerate((wq_ref, wk_ref, wv_ref)):
            r = jnp.dot(xv, w_ref[...], preferred_element_type=jnp.float32).astype(jnp.bfloat16)
            for kk in range(2):
                stage[p, kk, :, n * HEAD_DIM:(n + 1) * HEAD_DIM] = r[:, kk * HEAD_DIM:(kk + 1) * HEAD_DIM]
        for kk in range(2):
            here = c == 2 * i + kk

            @pl.when(jnp.logical_not(here))
            def _():
                y_send(p, kk, s, hf).start()

            @pl.when(here)
            def _():
                keep(p, kk, s, hf).start()
                share(p, kk, s, hf).start()

    def relay(p):
        s, hf = whose(p)

        @pl.when(main)
        def _():
            for d in range(1, cp):
                cc = lax.rem(c + d, cp)
                y_landed(cc, p, s, hf).wait_recv()
                pass_on(cc, p, s, hf).start()

    def step(p, _):
        u, w, hf = piece(p)
        for stage in range(1, 4):
            @pl.when(p == 4 * stage)
            def _():
                for v in range(2):
                    uu, _, hh = piece(4 * stage + v)
                    gather.landed(uu, 0, hh).wait_recv()
                    if stage == 1:
                        gather.relay(2 - uu).start()
                    gather.share(uu, hh).start()

        @pl.when(w == 1)
        def _():
            gather.landed(u, w, hf).wait_recv()

        s = source(u, w)
        project(xs[s, rows(hf), :], p, s, hf)

        @pl.when(p >= LAG)
        def _():
            relay(p - LAG)
        return 0

    lax.fori_loop(0, 16, step, 0)

    def tail(p, _):
        relay(p)
        return 0

    lax.fori_loop(16 - LAG, 16, tail, 0)
    gather.drain()

    def drain_pieces(p, _):
        s, hf = whose(p)
        for kk in range(2):
            here = c == 2 * i + kk

            @pl.when(jnp.logical_not(here))
            def _():
                y_send(p, kk, s, hf).wait_send()

            @pl.when(here)
            def _():
                keep(p, kk, s, hf).wait()

        @pl.when(main)
        def _():
            for cc in range(cp):
                pass_on(cc, p, s, hf).wait_send()

        @pl.when(jnp.logical_not(main))
        def _():
            for cc in range(cp):
                pass_on(cc, p, s, hf).wait_recv()
        return 0

    lax.fori_loop(0, 16, drain_pieces, 0)


def project_exchange(x, wq, wk, wv, cp, tp):
    seq = x.shape[0] * cp * tp
    hd = x.shape[1]
    anym = pl.BlockSpec(memory_space=pl.ANY)
    dma = pltpu.SemaphoreType.DMA
    return pl.pallas_call(
        functools.partial(project_kernel, cp, tp),
        out_shape=jax.ShapeDtypeStruct((seq, 3 * HEAD_DIM), jnp.bfloat16),
        in_specs=[anym] * 4,
        out_specs=anym,
        scratch_shapes=[
            pltpu.VMEM((tp,) + x.shape, jnp.bfloat16),
            pltpu.VMEM((16, 2, HALF, 3 * HEAD_DIM), jnp.bfloat16),
            pltpu.VMEM(wq.shape, jnp.bfloat16), pltpu.VMEM(wk.shape, jnp.bfloat16), pltpu.VMEM(wv.shape, jnp.bfloat16),
            dma((8,)), dma((8,)), dma((16,)), dma((32,)), dma((64,)), dma((64,)), dma((64,)), dma((16,)), dma((4,)),
        ],
        compiler_params=pltpu.CompilerParams(collective_id=0, has_side_effects=True, vmem_limit_bytes=62 << 20),
        name='project_exchange',
    )(x, wq, wk, wv)


QB = 256
KB = 1024


def q_block(g, i):
    return 4 * (g // 2) + (1 - i) * 3 * lax.rem(g, 2) + i * (1 + lax.rem(g, 2))


def attend_kernel(cp, tp, qkv_hbm, wo_hbm, x_hbm, h_ref, qkv_ref, wo, o_own, o_all, x_ref,
                  ss_w, ss_f, rs_w, ss, rs, sl, sq, sx):
    c = lax.axis_index('cp')
    t = lax.axis_index('tp')
    X = t // 2
    i = lax.rem(t, 2)
    head = X * cp + c
    nb = o_own.shape[0]
    nseg = nb // 2
    scale = HEAD_DIM ** -0.5 * LOG2E

    def seg_rows(j):
        return pl.ds(pl.multiple_of(j * KB, KB), KB)

    def load(j):
        return pltpu.make_async_copy(qkv_hbm.at[seg_rows(j)], qkv_ref.at[seg_rows(j)], sq.at[j])

    wrows = wo_hbm.shape[0]
    half = wrows // 2
    own_rows = pl.ds(pl.multiple_of(t * wrows, wrows), wrows)
    keep = pltpu.make_async_copy(wo_hbm, wo.at[own_rows], sx.at[0])
    keep.start()
    load_x = pltpu.make_async_copy(x_hbm, x_ref, sx.at[1])
    load_x.start()
    for j in range(nseg):
        load(j).start()
    greet(cp, tp, c, t)
    gather = Gather(
        cp, tp, c, t,
        lambda hf: wo_hbm.at[pl.ds(pl.multiple_of(hf * half, half), half)],
        lambda s, hf: wo.at[pl.ds(pl.multiple_of(s * wrows + hf * half, half), half)],
        ss_w, ss_f, rs_w)
    gather.start()

    def owner(g):
        b = q_block(g, i)
        seg = b // 4
        up = seg // cp
        return seg + up * (2 * cp - 1 - 2 * seg), lax.rem(b, 4) + 4 * up

    def cols(h):
        return pl.ds(pl.multiple_of(h * HEAD_DIM, HEAD_DIM), HEAD_DIM)

    def send(g):
        oc, ot = owner(g)
        return pltpu.make_async_remote_copy(
            src_ref=o_own.at[g], dst_ref=o_all.at[:, cols(head)], send_sem=ss.at[g], recv_sem=rs.at[head],
            device_id={'cp': oc, 'tp': ot}, device_id_type=MESH)

    def local(g):
        return pltpu.make_async_copy(o_own.at[g], o_all.at[:, cols(head)], sl)

    def mine(g):
        oc, ot = owner(g)
        return jnp.logical_and(oc == c, ot == t)

    def segment(seg, _):
        @pl.when(seg == nseg - 3)
        def _():
            for u in (1, 2):
                gather.landed(u, 0, 2 - u).wait_recv()
                gather.relay(2 - u).start()
                gather.share(u, 2 - u).start()

        @pl.when(seg == nseg - 2)
        def _():
            for u in (1, 2):
                gather.landed(u, 0, u - 1).wait_recv()
                gather.share(u, u - 1).start()

        load(seg).wait()
        blocks = [q_block(2 * seg + n, i) for n in range(2)]
        q = jnp.concatenate([qkv_ref[pl.ds(pl.multiple_of(b * QB, QB), QB), 0:HEAD_DIM] for b in blocks], axis=0)

        def chunk(j, m, l, acc, masked):
            k = qkv_ref[seg_rows(j), HEAD_DIM:2 * HEAD_DIM]
            v = qkv_ref[seg_rows(j), 2 * HEAD_DIM:3 * HEAD_DIM]
            s = lax.dot_general(q, k, (((1,), (1,)), ((), ())), preferred_element_type=jnp.float32) * scale
            if masked:
                row = lax.broadcasted_iota(jnp.int32, (2 * QB, KB), 0)
                qp = jnp.where(row < QB, blocks[0] * QB + row, (blocks[1] - 1) * QB + row)
                kp = j * KB + lax.broadcasted_iota(jnp.int32, (2 * QB, KB), 1)
                s = jnp.where(kp <= qp, s, NEG)
            mn = s[:, 0:128]
            for n in range(1, KB // 128):
                mn = jnp.maximum(mn, s[:, n * 128:(n + 1) * 128])
            mn = jnp.max(mn, axis=1, keepdims=True)
            if m is not None:
                mn = jnp.maximum(m, mn)
            w = jnp.exp2(s - mn)
            ls = w[:, 0:128]
            for n in range(1, KB // 128):
                ls = ls + w[:, n * 128:(n + 1) * 128]
            pv = jnp.dot(w.astype(jnp.bfloat16), v, preferred_element_type=jnp.float32)
            if m is None:
                return mn, ls, pv
            cc = jnp.exp2(m - mn)
            return mn, l * cc + ls, acc * cc + pv

        first = chunk(seg, None, None, None, True)
        m, l, acc = lax.fori_loop(0, seg, lambda j, carry: chunk(j, *carry, False), first)
        o = (acc / jnp.sum(l, axis=1, keepdims=True)).astype(jnp.bfloat16)
        for n in range(2):
            g = 2 * seg + n
            o_own[g] = o[n * QB:(n + 1) * QB]

            @pl.when(mine(g))
            def _():
                local(g).start()

            @pl.when(jnp.logical_not(mine(g)))
            def _():
                send(g).start()
        return 0

    lax.fori_loop(0, nseg, segment, 0)
    for hf in range(2):
        gather.landed(3, 0, hf).wait_recv()
        gather.share(3, hf).start()
    keep.wait()
    load_x.wait()
    for g in range(nb):
        @pl.when(mine(g))
        def _():
            local(g).wait()

        @pl.when(jnp.logical_not(mine(g)))
        def _():
            send(g).wait_send()
    core = lax.rem((lax.rem(t, 4) + 1) // 2, 2)
    for h in range(nb):
        here = jnp.logical_and(h == head, core == i)

        @pl.when(jnp.logical_not(here))
        def _():
            pltpu.make_async_remote_copy(
                src_ref=o_own.at[0], dst_ref=o_all.at[:, cols(h)], send_sem=ss.at[0], recv_sem=rs.at[h],
                device_id=gather.partner, device_id_type=MESH).wait_recv()
    for u in range(4):
        for hf in range(2):
            gather.landed(u, 1, hf).wait_recv()

    def column(n, _):
        at = pl.ds(pl.multiple_of(n * 256, 256), 256)
        att = jnp.dot(o_all[...], wo[:, at], preferred_element_type=jnp.float32)
        h_ref[:, at] = (x_ref[:, at].astype(jnp.float32) + att).astype(jnp.bfloat16)
        return 0

    lax.fori_loop(0, h_ref.shape[1] // 256, column, 0)
    gather.drain()


def attend(qkv, wo, x, cp, tp):
    seq = qkv.shape[0]
    nb = seq // QB // 2
    anym = pl.BlockSpec(memory_space=pl.ANY)
    dma = pltpu.SemaphoreType.DMA
    return pl.pallas_call(
        functools.partial(attend_kernel, cp, tp),
        out_shape=jax.ShapeDtypeStruct(x.shape, jnp.bfloat16),
        in_specs=[anym] * 3,
        out_specs=pl.BlockSpec(memory_space=pltpu.VMEM),
        scratch_shapes=[
            pltpu.VMEM(qkv.shape, jnp.bfloat16),
            pltpu.VMEM((tp * wo.shape[0], wo.shape[1]), jnp.bfloat16),
            pltpu.VMEM((nb, QB, HEAD_DIM), jnp.bfloat16),
            pltpu.VMEM((x.shape[0], nb * HEAD_DIM), jnp.bfloat16),
            pltpu.VMEM(x.shape, jnp.bfloat16),
            dma((8,)), dma((8,)), dma((16,)), dma((nb,)), dma((nb,)), dma, dma((nb // 2,)), dma((2,)),
        ],
        compiler_params=pltpu.CompilerParams(collective_id=1, has_side_effects=True, vmem_limit_bytes=62 << 20),
        name='attend',
    )(qkv, wo, x)


CHIPS = ((2, 2), (1, 0), (0, 1), (3, 0), (0, 3), (1, 1), (3, 3), (1, 3), (3, 1), (2, 0), (0, 2), (2, 1), (1, 2), (2, 3), (3, 2), (0, 0))
GROUP = 4


def experts_kernel(cp, tp, send_ref, wg_hbm, wu_hbm, wd_hbm, back_ref, recv, z, wg, wu, wd,
                   ss, rs, sb, rb, sw, sl):
    c = lax.axis_index('cp')
    t = lax.axis_index('tp')
    nx = tp // 2
    X = t // 2
    i = lax.rem(t, 2)
    me = c * tp + t
    n_dev = cp * tp
    offs = [(a, b, k) for a, b in CHIPS for k in range(2) if (a, b, k) != (0, 0, 0)]
    weights = [pltpu.make_async_copy(h, v, sw.at[n]) for n, (h, v) in enumerate(((wg_hbm, wg), (wu_hbm, wu), (wd_hbm, wd)))]
    for w in weights:
        w.start()
    greet(cp, tp, c, t)

    def target(o):
        s = 1 - 2 * i
        return lax.rem(c + s * o[0] + cp, cp), 2 * lax.rem(X + s * o[1] + nx, nx) + lax.rem(i + o[2], 2)

    def origin(o):
        j = lax.rem(i + o[2], 2)
        s = 1 - 2 * j
        return lax.rem(c - s * o[0] + cp, cp), 2 * lax.rem(X - s * o[1] + nx, nx) + j

    def out(k):
        pc, pt = target(offs[k])
        return pltpu.make_async_remote_copy(
            src_ref=send_ref.at[pc * tp + pt], dst_ref=recv.at[k], send_sem=ss.at[k], recv_sem=rs.at[k],
            device_id={'cp': pc, 'tp': pt}, device_id_type=MESH)

    def home(k):
        pc, pt = origin(offs[k])
        return pltpu.make_async_remote_copy(
            src_ref=z.at[k], dst_ref=back_ref.at[me], send_sem=sb.at[k], recv_sem=rb.at[k],
            device_id={'cp': pc, 'tp': pt}, device_id_type=MESH)

    last = n_dev - 1
    for k in range(last):
        out(k).start()
    own = pltpu.make_async_copy(send_ref.at[me], recv.at[last], sl.at[0])
    own.start()
    for w in weights:
        w.wait()
    cap, hd = recv.shape[1:]

    def group(n, _):
        for k in range(last):
            @pl.when(n == k // GROUP)
            def _():
                out(k).wait_recv()

        @pl.when(n == last // GROUP)
        def _():
            own.wait()

        rows = recv[pl.ds(n * GROUP, GROUP)].reshape(GROUP * cap, hd)
        gg = jnp.dot(rows, wg[...], preferred_element_type=jnp.float32)
        uu = jnp.dot(rows, wu[...], preferred_element_type=jnp.float32)
        act = (gg * jax.nn.sigmoid(gg) * uu).astype(jnp.bfloat16)
        r = jnp.dot(act, wd[...], preferred_element_type=jnp.float32).astype(jnp.bfloat16)
        z[pl.ds(n * GROUP, GROUP)] = r.reshape(GROUP, cap, hd)
        for k in range(last):
            @pl.when(n == k // GROUP)
            def _():
                home(k).start()
        return 0

    lax.fori_loop(0, n_dev // GROUP, group, 0)
    keep = pltpu.make_async_copy(z.at[last], back_ref.at[me], sl.at[1])
    keep.start()
    for k in range(last):
        out(k).wait_send()
    for k in range(last):
        home(k).wait_send()
        home(k).wait_recv()
    keep.wait()


def experts(send, wg, wu, wd, cp, tp):
    anym = pl.BlockSpec(memory_space=pl.ANY)
    dma = pltpu.SemaphoreType.DMA
    n = send.shape[0]
    return pl.pallas_call(
        functools.partial(experts_kernel, cp, tp),
        out_shape=jax.ShapeDtypeStruct(send.shape, jnp.bfloat16),
        in_specs=[pl.BlockSpec(memory_space=pltpu.VMEM), anym, anym, anym],
        out_specs=pl.BlockSpec(memory_space=pltpu.VMEM),
        scratch_shapes=[
            pltpu.VMEM(send.shape, jnp.bfloat16), pltpu.VMEM(send.shape, jnp.bfloat16),
            pltpu.VMEM(wg.shape, jnp.bfloat16), pltpu.VMEM(wu.shape, jnp.bfloat16), pltpu.VMEM(wd.shape, jnp.bfloat16),
            dma((n,)), dma((n,)), dma((n,)), dma((n,)), dma((3,)), dma((2,)),
        ],
        compiler_params=pltpu.CompilerParams(collective_id=2, has_side_effects=True, vmem_limit_bytes=60 << 20),
        name='experts',
    )(send, wg, wu, wd)


def routes(idx, ne, cap):
    t = idx.shape[0]
    e = jnp.arange(ne)[None, :]
    o0 = (idx[:, 0:1] == e).astype(jnp.bfloat16)
    o1 = (idx[:, 1:2] == e).astype(jnp.bfloat16)
    tri = (jnp.arange(t)[:, None] >= jnp.arange(t)[None, :]).astype(jnp.bfloat16)
    both = jnp.dot(tri, jnp.concatenate([o0, o1], axis=1), preferred_element_type=jnp.float32)
    c0 = both[:, :ne]
    c1 = both[:, ne:] + both[t - 1:, :ne]
    s0 = jnp.sum(o0.astype(jnp.float32) * c0, axis=1).astype(jnp.int32) - 1
    s1 = jnp.sum(o1.astype(jnp.float32) * c1, axis=1).astype(jnp.int32) - 1
    return idx[:, 0] * cap + s0, idx[:, 1] * cap + s1


def solution(mesh):
    cp = mesh.shape['cp']
    tp = mesh.shape['tp']
    ne = cp * tp
    rows_spec = P(('dp', 'cp', 'tp'), None)
    exp_spec = P(('cp', 'tp'), None, None)

    def local(x, idx, gates, wq, wk, wv, wo, w1g, w1u, w2):
        t, hd = x.shape
        cap = 4 * t // ne
        d0, d1 = routes(idx, ne, cap)
        qkv = project_exchange(x, wq, wk, wv, cp, tp)
        h = attend(qkv, wo, x, cp, tp)
        places = jnp.arange(ne * cap)
        pick = jnp.logical_or(places[:, None] == d0[None, :], places[:, None] == d1[None, :]).astype(jnp.bfloat16)
        send = jnp.dot(pick, h, preferred_element_type=jnp.float32).astype(jnp.bfloat16).reshape(ne, cap, hd)
        back = experts(send, w1g[0], w1u[0], w2[0], cp, tp).reshape(ne * cap, hd)
        z0 = jnp.dot((d0[:, None] == places[None, :]).astype(jnp.bfloat16), back, preferred_element_type=jnp.float32)
        z1 = jnp.dot((d1[:, None] == places[None, :]).astype(jnp.bfloat16), back, preferred_element_type=jnp.float32)
        y = h.astype(jnp.float32) + gates[:, 0:1] * z0 + gates[:, 1:2] * z1
        return y.astype(jnp.bfloat16)

    return jax.shard_map(local, mesh=mesh, in_specs=(rows_spec, rows_spec, rows_spec, P(None, 'tp'), P(None, 'tp'), P(None, 'tp'), P('tp', None), exp_spec, exp_spec, exp_spec), out_specs=rows_spec, check_vma=False)
```

time: 281 us -> 244 us (0.87)
  Pallas kernels: 242 us -> 228 us
  between operations: 13.6 us -> 0.11 us
  local copies, waits for them, and re-layouts: 6.1 us -> 1.01 us
  matrix products: 15.6 us -> 10.7 us
    pallas_call x1, Pallas kernels: 64.6 us -> 57.6 us  [project_exchange(): pl.pallas_call(functools.partial(project_kernel, cp, tp), out_shape=jax.S...]
    dot_general x1 -> x0, matrix products: 6.07 us -> none  [local(): att = jnp.dot(o, wo_all, preferred_element_type=jnp.float32)]
    unnamed x18 -> x8, local copies, waits for them, and re-layouts: 5.89 us -> 0.03 us
    pallas_call x1, Pallas kernels: 113 us -> 108 us  [experts(): pl.pallas_call(functools.partial(experts_kernel, cp, tp), out_shape=jax.S...]
    pallas_call x2 -> x1, Pallas kernels: 64.1 us -> 62.8 us  [attend(): pl.pallas_call(functools.partial(attend_kernel, cp, tp), out_shape=jax.Sh...]
  transfers between devices with their start and end apart: 1 -> 0, of which waited for: 0 -> 0; matrix products, arithmetic and copies ran while one was open for 0% -> 0% of each run, Pallas kernels for 23% -> 0%
where the time goes in v3:
time: 244 us; the launch traced here: 240 us
  Pallas kernels  228 us (93%)
  matrix products  10.7 us (4%)
    pallas_call x1, Pallas kernels, experts(): pl.pallas_call(functools.partial(experts_kernel, cp, tp), out_shape=jax.S...  108 us
    pallas_call x1, Pallas kernels, attend(): pl.pallas_call(functools.partial(attend_kernel, cp, tp), out_shape=jax.Sh...  62.8 us
    pallas_call x1, Pallas kernels, project_exchange(): pl.pallas_call(functools.partial(project_kernel, cp, tp), out_shape=jax.S...  57.6 us

profile of v3, /device:TPU:103, one launch (start us, length us, event | category | flops | bytes accessed | tf_op | source)
XLA Modules:
  0.0 240.0 jit_solution(6329557286174161545)
XLA Ops:
  0.0 0.8 fusion.20
  0.8 0.2 fusion.9
  0.9 0.2 slice_reduce_fusion
  1.1 0.1 fusion.12
  1.3 57.6 %project_exchange.1.qkv_hbm = bf16[8192,384]{1,0:T(8,128)(2,1)} custom-call(bf16[256,2048]{1,0:T(8,128)(2,1)} %x_hbm.3, bf16[2048,256]{1,0:T(8,128)(2,1)} %wq_hbm.1, bf16[2048,256]{1,0:T(8,128)(2,1)} %wk_hbm.1, bf16[2048,256]{1,0:T(8,128)(2,1)} %wv_hbm.1), custom_call_target="tpu_custom_call" | custom-call | tf_op jit(solution)/shard_map/project_exchange/pallas_call | solution.py:238
  58.9 62.8 %attend.1 = bf16[256,2048]{1,0:T(8,128)(2,1)} custom-call(bf16[8192,384]{1,0:T(8,128)(2,1)} %project_exchange.1.qkv_hbm, bf16[256,2048]{1,0:T(8,128)(2,1)} %wo_hbm.1, bf16[256,2048]{1,0:T(8,128)(2,1)} %x_hbm.3), custom_call_target="tpu_custom_call" | custom-call | tf_op jit(solution)/shard_map/attend/pallas_call | solution.py:419
  121.7 4.4 %convolution_convert_fusion = bf16[1024,2048]{1,0:T(8,128)(2,1)} fusion(bf16[256,2048]{1,0:T(8,128)(2,1)} %attend.1, s32[256]{0:T(256)S(1)} %get-tuple-element.16, s32[256]{0:T(256)S(1)} %get-tuple-element.14), kind=kOutput, calls=%fused_computation | convolution fusion | flops 1076625408 | bytes 5244928 | tf_op jit(solution)/shard_map/dot_general | solution.py:567
  126.1 0.0 copy-start.2
  126.1 0.0 copy-start.3
  126.1 107.6 %experts.1 = bf16[32,32,2048]{2,1,0:T(8,128)(2,1)} custom-call(bf16[32,32,2048]{2,1,0:T(8,128)(2,1)} %bitcast.16, bf16[2048,1408]{1,0:T(8,128)(2,1)} %bitcast.17, bf16[2048,1408]{1,0:T(8,128)(2,1)} %bitcast.18, bf16[1408,2048]{1,0:T(8,128)(2,1)} %bitcast.19), custom_call_target="tpu_custom_call" | custom-call | tf_op jit(solution)/shard_map/experts/pallas_call | solution.py:523
  233.7 0.0 copy-start
  233.7 0.0 copy-start.1
  233.8 0.0 copy-done.2
  233.8 0.0 copy-done.3
  233.8 3.6 %convolution_multiply_fusion = f32[256,2048]{1,0:T(8,128)S(1)} fusion(bf16[1024,2048]{1,0:T(8,128)(2,1)} %bitcast.20, f32[256]{0:T(256)S(1)} %bitcast.33, s32[256]{0:T(256)S(1)} %bitcast.32), kind=kOutput, calls=%fused_computation.1 | convolution fusion | flops 1074528256 | bytes 6293504 | tf_op jit(solution)/shard_map/dot_general | solution.py:570
  237.4 0.0 copy-done
  237.5 0.0 copy-done.1
  237.5 2.5 %fusion.2 = bf16[256,2048]{1,0:T(8,128)(2,1)} fusion(f32[256,2048]{1,0:T(8,128)S(1)} %convolution_multiply_fusion, bf16[1024,2048]{1,0:T(8,128)(2,1)S(1)} %bitcast.21, bf16[256,2048]{1,0:T(8,128)(2,1)S(1)} %copy-done.1, f32[256]{0:T(256)S(1)} %bitcast.31, s32[256]{0:T(256)S(1)} %bitcast.30), kind=kOutput, calls=%fused_computation.5 | convolution fusion | flops 1076625408 | bytes 8390656 | tf_op jit(solution)/shard_map/dot_general | solution.py:569
  (5 shorter events, 0.0 us)
Async XLA Ops:
  126.1 107.7 %copy-start.2 = (s32[256,2]{0,1:T(2,128)S(1)}, s32[256,2]{0,1:T(2,128)}, u32[]{:S(2)}) copy-start(s32[256,2]{0,1:T(2,128)} %param.11) | copy-start | bytes 6148
  126.1 107.7 %copy-start.3 = (f32[256,2]{0,1:T(2,128)S(1)}, f32[256,2]{0,1:T(2,128)}, u32[]{:S(2)}) copy-start(f32[256,2]{0,1:T(2,128)} %param.12) | copy-start | bytes 6148
  233.7 3.7 %copy-start = (bf16[32,32,2048]{2,1,0:T(8,128)(2,1)S(1)}, bf16[32,32,2048]{2,1,0:T(8,128)(2,1)}, u32[]{:S(2)}) copy-start(bf16[32,32,2048]{2,1,0:T(8,128)(2,1)} %experts.1) | copy-start | bytes 12582916
  233.7 3.7 %copy-start.1 = (bf16[256,2048]{1,0:T(8,128)(2,1)S(1)}, bf16[256,2048]{1,0:T(8,128)(2,1)}, u32[]{:S(2)}) copy-start(bf16[256,2048]{1,0:T(8,128)(2,1)} %attend.1) | copy-start | bytes 3145732

commit v4 on v3

v4 whole, which is shorter than its diff:
```python
import functools

import jax
import jax.numpy as jnp
from jax import lax
from jax.experimental import pallas as pl
from jax.experimental.pallas import tpu as pltpu
from jax.sharding import PartitionSpec as P

HEAD_DIM = 128
NEG = -1e30
LOG2E = 1.4426950408889634
MESH = pl.DeviceIdType.MESH
PIECE = 64
LAG = 4


ORDER = (
    (2, 2, 0), (2, 2, 1), (1, 0, 0), (1, 0, 1), (0, 1, 0), (0, 1, 1), (3, 0, 0), (3, 0, 1),
    (0, 3, 0), (0, 3, 1), (1, 1, 0), (1, 1, 1), (3, 3, 0), (3, 3, 1), (1, 3, 0), (1, 3, 1),
    (3, 1, 0), (3, 1, 1), (2, 0, 0), (2, 0, 1), (0, 2, 0), (0, 2, 1), (2, 1, 0), (2, 1, 1),
    (1, 2, 0), (1, 2, 1), (2, 3, 0), (2, 3, 1), (3, 2, 0), (3, 2, 1), (0, 0, 1),
)


def target(o, cp, nx, c, t):
    X, i = t // 2, lax.rem(t, 2)
    s = 1 - 2 * i
    return lax.rem(c + s * o[0] + cp, cp), 2 * lax.rem(X + s * o[1] + nx, nx) + lax.rem(i + o[2], 2)


def origin(o, cp, nx, c, t):
    X, j = t // 2, lax.rem(t + o[2], 2)
    s = 1 - 2 * j
    return lax.rem(c - s * o[0] + cp, cp), 2 * lax.rem(X - s * o[1] + nx, nx) + j


def greet(cp, tp, c, t):
    sem = pltpu.get_barrier_semaphore()
    n = 0
    for dc in range(cp):
        for dt in range(tp):
            if dc or dt:
                peer = {'cp': lax.rem(c + dc, cp), 'tp': lax.rem(t + dt, tp)}
                pl.semaphore_signal(sem, inc=1, device_id=peer, device_id_type=MESH)
                n += 1
    pl.semaphore_wait(sem, n)


class Gather:
    def __init__(self, np, cp, tp, c, t, src, dst, send, relayed, passed, recv):
        self.np, self.c, self.t, self.nx = np, c, t, tp // 2
        self.X, self.i = t // 2, lax.rem(t, 2)
        self.partner = {'cp': c, 'tp': 2 * self.X + 1 - self.i}
        self.src, self.dst = src, dst
        self.send, self.relayed, self.passed, self.recv = send, relayed, passed, recv

    def chip(self, d):
        return {'cp': self.c, 'tp': 2 * lax.rem(self.X + d, self.nx) + self.i}

    def source(self, u, w):
        dx = u + (u // 2) * (5 - 2 * u)
        return 2 * lax.rem(self.X + dx, self.nx) + lax.rem(self.i + w, 2)

    def copy(self, src, dst, send, u, w, pc, dev):
        return pltpu.make_async_remote_copy(
            src_ref=src, dst_ref=dst, send_sem=send, recv_sem=self.recv.at[(u * 2 + w) * self.np + pc],
            device_id=dev, device_id_type=MESH)

    def own(self, d, pc):
        dev, u, w = {0: (self.partner, 0, 1), 1: (self.chip(1), 2, 0), 2: (self.chip(3), 1, 0)}[d]
        return self.copy(self.src(pc), self.dst(self.t, pc), self.send.at[d * self.np + pc], u, w, pc, dev)

    def relay(self, pc):
        back = pc // (self.np // 2)
        ref = self.dst(self.source(2 - back, 0), pc)
        return self.copy(ref, ref, self.relayed.at[pc], 3, 0, pc, self.chip(1 + 2 * back))

    def share(self, u, pc):
        ref = self.dst(self.source(u, 0), pc)
        return self.copy(ref, ref, self.passed.at[(u - 1) * self.np + pc], u, 1, pc, self.partner)

    def landed(self, u, w, pc):
        ref = self.dst(self.source(u, w), pc)
        return self.copy(ref, ref, self.passed.at[0], u, w, pc, self.partner)

    def start(self):
        for n in range(self.np):
            self.own(1, n).start()
            self.own(2, self.np - 1 - n).start()
            self.own(0, n).start()

    def drain(self):
        for pc in range(self.np):
            for d in range(3):
                self.own(d, pc).wait_send()
            self.relay(pc).wait_send()
            for u in range(1, 4):
                self.share(u, pc).wait_send()

    @staticmethod
    def semaphores(np):
        dma = pltpu.SemaphoreType.DMA
        return [dma((3 * np,)), dma((np,)), dma((3 * np,)), dma((8 * np,))]


def route(cp, tp, c, t, idx_ref, place_ref, turned_ref):
    n_dev = cp * tp
    rows, choices = idx_ref.shape[1], 2
    cap = 2 * choices * rows // n_dev
    names = jnp.where(lax.broadcasted_iota(jnp.int32, idx_ref.shape, 0) < choices, idx_ref[...], 0).astype(jnp.float32).T
    lane = lax.broadcasted_iota(jnp.int32, (rows, 128), 1)
    named = [(lane.astype(jnp.float32) == names[:, n:n + 1]).astype(jnp.float32) for n in range(choices)]
    tri = (lax.broadcasted_iota(jnp.int32, (rows, rows), 0) >= lax.broadcasted_iota(jnp.int32, (rows, rows), 1))
    count = jnp.dot(tri.astype(jnp.float32).astype(jnp.bfloat16), jnp.concatenate(named, axis=1).astype(jnp.bfloat16),
                    preferred_element_type=jnp.float32)
    one = lax.broadcasted_iota(jnp.int32, (8, 128), 1)
    base = jnp.where(one == c * tp + t, float((n_dev - 1) * cap), 0.0)
    for k, o in enumerate(ORDER):
        pc, pt = target(o, cp, tp // 2, c, t)
        base = jnp.where(one == pc * tp + pt, float(k * cap), base)
    base = base[0:1, :]
    later = base + count[rows - 1:rows, :128]
    p0 = jnp.sum(named[0] * (count[:, :128] + base), axis=1, keepdims=True) - 1.0
    p1 = jnp.sum(named[1] * (count[:, 128:] + later), axis=1, keepdims=True) - 1.0
    both = jnp.where(lane == 0, p0, jnp.where(lane == 1, p1, 0.0))
    place_ref[...] = both
    turned_ref[...] = both.T[:8, :]


def project_kernel(cp, tp, x_hbm, idx_hbm, wq_hbm, wk_hbm, wv_hbm, out_ref, place_ref, turned_ref, xs, stage, wq_ref, wk_ref, wv_ref, idx_ref,
                   ss_x, sr_x, ss_f, rs_x, sy, ry, sf, rf, sl, sw):
    c = lax.axis_index('cp')
    t = lax.axis_index('tp')
    X = t // 2
    i = lax.rem(t, 2)
    partner = {'cp': c, 'tp': 2 * X + 1 - i}
    main = i == c // 2
    loads = [pltpu.make_async_copy(h, v, sw.at[n]) for n, (h, v) in enumerate(
        ((x_hbm, xs.at[t]), (wq_hbm, wq_ref), (wk_hbm, wk_ref), (wv_hbm, wv_ref), (idx_hbm, idx_ref.at[0:2])))]
    for load in loads:
        load.start()
    greet(cp, tp, c, t)

    np = x_hbm.shape[0] // PIECE
    total = tp * np

    def rows(hf):
        return pl.ds(pl.multiple_of(hf * PIECE, PIECE), PIECE)

    gather = Gather(
        np, cp, tp, c, t, lambda hf: x_hbm.at[rows(hf)], lambda s, hf: xs.at[s, rows(hf)], ss_x, sr_x, ss_f, rs_x)
    source = gather.source

    def place(cc, s, hf):
        seg = cc + (s // (tp // 2)) * (2 * cp - 1 - 2 * cc)
        return pl.ds(pl.multiple_of((seg * (tp // 2) + lax.rem(s, tp // 2)) * (np * PIECE) + hf * PIECE, PIECE), PIECE)

    def piece(p):
        eighth = p // 8
        own, opp = 1 - (eighth + 3) // 4, eighth // 3
        mid = 1 - own - opp
        k = p // 4 - 2
        v = lax.rem(p, 2)
        w = own * (p // 4) + (1 - own) * (lax.rem(p, 4) // 2)
        pc = own * lax.rem(p, 4) + mid * ((1 - v) * (3 - k) + v * k) + opp * ((1 - v) * (k - 4) + v * (7 - k))
        return mid * (1 + v) + 3 * opp, w, pc

    def whose(p):
        u, w, hf = piece(p)
        return source(u, w), hf

    def y_send(p, kk, s, hf):
        return pltpu.make_async_remote_copy(
            src_ref=stage.at[p, kk], dst_ref=out_ref.at[place(c, s, hf)],
            send_sem=sy.at[p * 2 + kk], recv_sem=ry.at[c * total + p],
            device_id={'cp': 2 * i + kk, 'tp': t}, device_id_type=MESH)

    def keep(p, kk, s, hf):
        return pltpu.make_async_copy(stage.at[p, kk], out_ref.at[place(c, s, hf)], sl.at[p])

    def share(p, kk, s, hf):
        return pltpu.make_async_remote_copy(
            src_ref=stage.at[p, kk], dst_ref=out_ref.at[place(c, s, hf)],
            send_sem=sf.at[c * total + p], recv_sem=rf.at[c * total + p],
            device_id=partner, device_id_type=MESH)

    def pass_on(cc, p, s, hf):
        return pltpu.make_async_remote_copy(
            src_ref=out_ref.at[place(cc, s, hf)], dst_ref=out_ref.at[place(cc, s, hf)],
            send_sem=sf.at[cc * total + p], recv_sem=rf.at[cc * total + p],
            device_id=partner, device_id_type=MESH)

    def y_landed(cc, p, s, hf):
        return pltpu.make_async_remote_copy(
            src_ref=out_ref.at[place(cc, s, hf)], dst_ref=out_ref.at[place(cc, s, hf)],
            send_sem=sf.at[cc * total + p], recv_sem=ry.at[cc * total + p],
            device_id=partner, device_id_type=MESH)

    gather.start()
    for load in loads:
        load.wait()
    route(cp, tp, c, t, idx_ref, place_ref, turned_ref)

    def project(xv, p, s, hf):
        for n, w_ref in enumerate((wq_ref, wk_ref, wv_ref)):
            r = jnp.dot(xv, w_ref[...], preferred_element_type=jnp.float32).astype(jnp.bfloat16)
            for kk in range(2):
                stage[p, kk, :, n * HEAD_DIM:(n + 1) * HEAD_DIM] = r[:, kk * HEAD_DIM:(kk + 1) * HEAD_DIM]
        for kk in range(2):
            here = c == 2 * i + kk

            @pl.when(jnp.logical_not(here))
            def _():
                y_send(p, kk, s, hf).start()

            @pl.when(here)
            def _():
                keep(p, kk, s, hf).start()
                share(p, kk, s, hf).start()

    def relay(p):
        s, hf = whose(p)

        @pl.when(main)
        def _():
            for d in range(1, cp):
                cc = lax.rem(c + d, cp)
                y_landed(cc, p, s, hf).wait_recv()
                pass_on(cc, p, s, hf).start()

    def step(p, _):
        u, w, hf = piece(p)
        for first in range(8, total, 4):
            @pl.when(p == first)
            def _():
                for v in range(2):
                    uu, _, pc = piece(first + v)
                    gather.landed(uu, 0, pc).wait_recv()
                    if first < 16:
                        gather.relay(pc).start()
                    gather.share(uu, pc).start()

        @pl.when(w == 1)
        def _():
            gather.landed(u, w, hf).wait_recv()

        s = source(u, w)
        project(xs[s, rows(hf), :], p, s, hf)

        @pl.when(p >= LAG)
        def _():
            relay(p - LAG)
        return 0

    lax.fori_loop(0, total, step, 0)

    def tail(p, _):
        relay(p)
        return 0

    lax.fori_loop(total - LAG, total, tail, 0)
    gather.drain()

    def drain_pieces(p, _):
        s, hf = whose(p)
        for kk in range(2):
            here = c == 2 * i + kk

            @pl.when(jnp.logical_not(here))
            def _():
                y_send(p, kk, s, hf).wait_send()

            @pl.when(here)
            def _():
                keep(p, kk, s, hf).wait()

        @pl.when(main)
        def _():
            for cc in range(cp):
                pass_on(cc, p, s, hf).wait_send()

        @pl.when(jnp.logical_not(main))
        def _():
            for cc in range(cp):
                pass_on(cc, p, s, hf).wait_recv()
        return 0

    lax.fori_loop(0, total, drain_pieces, 0)


def project_exchange(x, idx, wq, wk, wv, cp, tp):
    seq = x.shape[0] * cp * tp
    np = x.shape[0] // PIECE
    total = tp * np
    anym = pl.BlockSpec(memory_space=pl.ANY)
    dma = pltpu.SemaphoreType.DMA
    return pl.pallas_call(
        functools.partial(project_kernel, cp, tp),
        out_shape=(
            jax.ShapeDtypeStruct((seq, 3 * HEAD_DIM), jnp.bfloat16),
            jax.ShapeDtypeStruct((x.shape[0], 128), jnp.float32),
            jax.ShapeDtypeStruct((8, x.shape[0]), jnp.float32),
        ),
        in_specs=[anym] * 5,
        out_specs=(anym, pl.BlockSpec(memory_space=pltpu.VMEM), pl.BlockSpec(memory_space=pltpu.VMEM)),
        scratch_shapes=[
            pltpu.VMEM((tp,) + x.shape, jnp.bfloat16),
            pltpu.VMEM((total, 2, PIECE, 3 * HEAD_DIM), jnp.bfloat16),
            pltpu.VMEM(wq.shape, jnp.bfloat16), pltpu.VMEM(wk.shape, jnp.bfloat16), pltpu.VMEM(wv.shape, jnp.bfloat16),
            pltpu.VMEM((8, x.shape[0]), jnp.int32),
            *Gather.semaphores(np),
            dma((2 * total,)), dma((cp * total,)), dma((cp * total,)), dma((cp * total,)), dma((total,)), dma((5,)),
        ],
        compiler_params=pltpu.CompilerParams(collective_id=0, has_side_effects=True, vmem_limit_bytes=62 << 20),
        name='project_exchange',
    )(x, idx.T, wq, wk, wv)


QB = 256
KB = 1024


def q_block(g, i):
    return 4 * (g // 2) + (1 - i) * 3 * lax.rem(g, 2) + i * (1 + lax.rem(g, 2))


def attend_kernel(cp, tp, qkv_hbm, wo_hbm, x_hbm, h_ref, qkv_ref, wo, o_own, o_all, x_ref,
                  ss_w, sr_w, ss_f, rs_w, ss, rs, sl, sq, sx):
    c = lax.axis_index('cp')
    t = lax.axis_index('tp')
    X = t // 2
    i = lax.rem(t, 2)
    head = X * cp + c
    nb = o_own.shape[0]
    nseg = nb // 2
    scale = HEAD_DIM ** -0.5 * LOG2E

    def seg_rows(j):
        return pl.ds(pl.multiple_of(j * KB, KB), KB)

    def load(j):
        return pltpu.make_async_copy(qkv_hbm.at[seg_rows(j)], qkv_ref.at[seg_rows(j)], sq.at[j])

    wrows = wo_hbm.shape[0]
    half = wrows // 2
    own_rows = pl.ds(pl.multiple_of(t * wrows, wrows), wrows)
    keep = pltpu.make_async_copy(wo_hbm, wo.at[own_rows], sx.at[0])
    keep.start()
    load_x = pltpu.make_async_copy(x_hbm, x_ref, sx.at[1])
    load_x.start()
    for j in range(nseg):
        load(j).start()
    greet(cp, tp, c, t)
    gather = Gather(
        2, cp, tp, c, t,
        lambda hf: wo_hbm.at[pl.ds(pl.multiple_of(hf * half, half), half)],
        lambda s, hf: wo.at[pl.ds(pl.multiple_of(s * wrows + hf * half, half), half)],
        ss_w, sr_w, ss_f, rs_w)
    gather.start()

    def owner(g):
        b = q_block(g, i)
        seg = b // 4
        up = seg // cp
        return seg + up * (2 * cp - 1 - 2 * seg), lax.rem(b, 4) + 4 * up

    def cols(h):
        return pl.ds(pl.multiple_of(h * HEAD_DIM, HEAD_DIM), HEAD_DIM)

    def send(g):
        oc, ot = owner(g)
        return pltpu.make_async_remote_copy(
            src_ref=o_own.at[g], dst_ref=o_all.at[:, cols(head)], send_sem=ss.at[g], recv_sem=rs.at[head],
            device_id={'cp': oc, 'tp': ot}, device_id_type=MESH)

    def local(g):
        return pltpu.make_async_copy(o_own.at[g], o_all.at[:, cols(head)], sl)

    def mine(g):
        oc, ot = owner(g)
        return jnp.logical_and(oc == c, ot == t)

    def segment(seg, _):
        @pl.when(seg == nseg - 3)
        def _():
            for u in (1, 2):
                gather.landed(u, 0, 2 - u).wait_recv()
                gather.relay(2 - u).start()
                gather.share(u, 2 - u).start()

        @pl.when(seg == nseg - 2)
        def _():
            for u in (1, 2):
                gather.landed(u, 0, u - 1).wait_recv()
                gather.share(u, u - 1).start()

        load(seg).wait()
        blocks = [q_block(2 * seg + n, i) for n in range(2)]
        q = jnp.concatenate([qkv_ref[pl.ds(pl.multiple_of(b * QB, QB), QB), 0:HEAD_DIM] for b in blocks], axis=0)

        def chunk(j, m, l, acc, masked):
            k = qkv_ref[seg_rows(j), HEAD_DIM:2 * HEAD_DIM]
            v = qkv_ref[seg_rows(j), 2 * HEAD_DIM:3 * HEAD_DIM]
            s = lax.dot_general(q, k, (((1,), (1,)), ((), ())), preferred_element_type=jnp.float32) * scale
            if masked:
                row = lax.broadcasted_iota(jnp.int32, (2 * QB, KB), 0)
                qp = jnp.where(row < QB, blocks[0] * QB + row, (blocks[1] - 1) * QB + row)
                kp = j * KB + lax.broadcasted_iota(jnp.int32, (2 * QB, KB), 1)
                s = jnp.where(kp <= qp, s, NEG)
            mn = s[:, 0:128]
            for n in range(1, KB // 128):
                mn = jnp.maximum(mn, s[:, n * 128:(n + 1) * 128])
            mn = jnp.max(mn, axis=1, keepdims=True)
            if m is not None:
                mn = jnp.maximum(m, mn)
            w = jnp.exp2(s - mn)
            ls = w[:, 0:128]
            for n in range(1, KB // 128):
                ls = ls + w[:, n * 128:(n + 1) * 128]
            pv = jnp.dot(w.astype(jnp.bfloat16), v, preferred_element_type=jnp.float32)
            if m is None:
                return mn, ls, pv
            cc = jnp.exp2(m - mn)
            return mn, l * cc + ls, acc * cc + pv

        first = chunk(seg, None, None, None, True)
        m, l, acc = lax.fori_loop(0, seg, lambda j, carry: chunk(j, *carry, False), first)
        o = (acc / jnp.sum(l, axis=1, keepdims=True)).astype(jnp.bfloat16)
        for n in range(2):
            g = 2 * seg + n
            o_own[g] = o[n * QB:(n + 1) * QB]

            @pl.when(mine(g))
            def _():
                local(g).start()

            @pl.when(jnp.logical_not(mine(g)))
            def _():
                send(g).start()
        return 0

    lax.fori_loop(0, nseg, segment, 0)
    for hf in range(2):
        gather.landed(3, 0, hf).wait_recv()
        gather.share(3, hf).start()
    keep.wait()
    load_x.wait()
    for g in range(nb):
        @pl.when(mine(g))
        def _():
            local(g).wait()

        @pl.when(jnp.logical_not(mine(g)))
        def _():
            send(g).wait_send()
    core = lax.rem((lax.rem(t, 4) + 1) // 2, 2)
    for h in range(nb):
        here = jnp.logical_and(h == head, core == i)

        @pl.when(jnp.logical_not(here))
        def _():
            pltpu.make_async_remote_copy(
                src_ref=o_own.at[0], dst_ref=o_all.at[:, cols(h)], send_sem=ss.at[0], recv_sem=rs.at[h],
                device_id=gather.partner, device_id_type=MESH).wait_recv()
    for u in range(4):
        for hf in range(2):
            gather.landed(u, 1, hf).wait_recv()

    def column(n, _):
        at = pl.ds(pl.multiple_of(n * 256, 256), 256)
        att = jnp.dot(o_all[...], wo[:, at], preferred_element_type=jnp.float32)
        h_ref[:, at] = (x_ref[:, at].astype(jnp.float32) + att).astype(jnp.bfloat16)
        return 0

    lax.fori_loop(0, h_ref.shape[1] // 256, column, 0)
    gather.drain()


def attend(qkv, wo, x, cp, tp):
    seq = qkv.shape[0]
    nb = seq // QB // 2
    anym = pl.BlockSpec(memory_space=pl.ANY)
    dma = pltpu.SemaphoreType.DMA
    return pl.pallas_call(
        functools.partial(attend_kernel, cp, tp),
        out_shape=jax.ShapeDtypeStruct(x.shape, jnp.bfloat16),
        in_specs=[anym] * 3,
        out_specs=pl.BlockSpec(memory_space=pltpu.VMEM),
        scratch_shapes=[
            pltpu.VMEM(qkv.shape, jnp.bfloat16),
            pltpu.VMEM((tp * wo.shape[0], wo.shape[1]), jnp.bfloat16),
            pltpu.VMEM((nb, QB, HEAD_DIM), jnp.bfloat16),
            pltpu.VMEM((x.shape[0], nb * HEAD_DIM), jnp.bfloat16),
            pltpu.VMEM(x.shape, jnp.bfloat16),
            *Gather.semaphores(2), dma((nb,)), dma((nb,)), dma, dma((nb // 2,)), dma((2,)),
        ],
        compiler_params=pltpu.CompilerParams(collective_id=1, has_side_effects=True, vmem_limit_bytes=62 << 20),
        name='attend',
    )(qkv, wo, x)


GROUP = 4
PICK = 4
PUT = 4


def experts_kernel(cp, tp, turned_hbm, place_hbm, gates_hbm, h_ref, wg_hbm, wu_hbm, wd_hbm, out_ref,
                   send, recv, z, back, wg, wu, wd, d_row, d_col, gates_ref, y_ref,
                   ss, rs, sb, rb, sw, sl):
    c = lax.axis_index('cp')
    t = lax.axis_index('tp')
    nx = tp // 2
    X = t // 2
    i = lax.rem(t, 2)
    me = c * tp + t
    n_dev = cp * tp
    cap, hd = recv.shape[1:]
    rows = h_ref.shape[0]
    last = n_dev - 1
    small = [pltpu.make_async_copy(h, v, sw.at[3 + n]) for n, (h, v) in enumerate(
        ((turned_hbm, d_row), (place_hbm, d_col), (gates_hbm, gates_ref.at[0:2])))]
    weights = [pltpu.make_async_copy(h, v, sw.at[n]) for n, (h, v) in enumerate(((wg_hbm, wg), (wu_hbm, wu), (wd_hbm, wd)))]
    for w in small + weights:
        w.start()
    for w in small:
        w.wait()

    def out(k):
        pc, pt = target(ORDER[k], cp, nx, c, t)
        return pltpu.make_async_remote_copy(
            src_ref=send.at[k], dst_ref=recv.at[k], send_sem=ss.at[k], recv_sem=rs.at[k],
            device_id={'cp': pc, 'tp': pt}, device_id_type=MESH)

    def home(k):
        pc, pt = origin(ORDER[k], cp, nx, c, t)
        return pltpu.make_async_remote_copy(
            src_ref=z.at[k], dst_ref=back.at[k], send_sem=sb.at[k], recv_sem=rb.at[k],
            device_id={'cp': pc, 'tp': pt}, device_id_type=MESH)

    def places(n, blocks, axis, shape):
        return (n * blocks * cap + lax.broadcasted_iota(jnp.int32, shape, axis)).astype(jnp.float32)

    def select(n, _):
        at = places(n, PICK, 0, (PICK * cap, rows))
        pick = jnp.logical_or(at == d_row[0:1, :], at == d_row[1:2, :]).astype(jnp.float32).astype(jnp.bfloat16)
        r = jnp.dot(pick, h_ref[...], preferred_element_type=jnp.float32).astype(jnp.bfloat16)
        send[pl.ds(n * PICK, PICK)] = r.reshape(PICK, cap, hd)

        @pl.when(n == 0)
        def _():
            greet(cp, tp, c, t)

        for k in range(last):
            @pl.when(n == k // PICK)
            def _():
                out(k).start()
        return 0

    lax.fori_loop(0, n_dev // PICK, select, 0)
    own = pltpu.make_async_copy(send.at[last], recv.at[last], sl.at[0])
    own.start()
    for w in weights:
        w.wait()

    def group(n, _):
        for k in range(last):
            @pl.when(n == k // GROUP)
            def _():
                out(k).wait_recv()

        @pl.when(n == last // GROUP)
        def _():
            own.wait()

        xr = recv[pl.ds(n * GROUP, GROUP)].reshape(GROUP * cap, hd)
        gg = jnp.dot(xr, wg[...], preferred_element_type=jnp.float32)
        uu = jnp.dot(xr, wu[...], preferred_element_type=jnp.float32)
        act = (gg * jax.nn.sigmoid(gg) * uu).astype(jnp.bfloat16)
        r = jnp.dot(act, wd[...], preferred_element_type=jnp.float32).astype(jnp.bfloat16)
        z[pl.ds(n * GROUP, GROUP)] = r.reshape(GROUP, cap, hd)
        for k in range(last):
            @pl.when(n == k // GROUP)
            def _():
                home(k).start()
        return 0

    lax.fori_loop(0, n_dev // GROUP, group, 0)
    keep = pltpu.make_async_copy(z.at[last], back.at[last], sl.at[1])
    keep.start()
    y_ref[...] = h_ref[...].astype(jnp.float32)
    gates = jnp.where(lax.broadcasted_iota(jnp.int32, gates_ref.shape, 0) < 2, gates_ref[...], 0.0).T
    for k in range(last):
        out(k).wait_send()

    def combine(n, _):
        for k in range(last):
            @pl.when(n == k // PUT)
            def _():
                home(k).wait_recv()

        @pl.when(n == last // PUT)
        def _():
            keep.wait()

        at = places(n, PUT, 1, (rows, PUT * cap))
        blk = back[pl.ds(n * PUT, PUT)].reshape(PUT * cap, hd)
        total = y_ref[...]
        for choice in range(2):
            put = (at == d_col[:, choice:choice + 1]).astype(jnp.float32).astype(jnp.bfloat16)
            zz = jnp.dot(put, blk, preferred_element_type=jnp.float32)
            total = total + gates[:, choice:choice + 1] * zz
        y_ref[...] = total
        return 0

    lax.fori_loop(0, n_dev // PUT, combine, 0)
    out_ref[...] = y_ref[...].astype(jnp.bfloat16)
    for k in range(last):
        home(k).wait_send()


def experts(place, turned, gates, h, wg, wu, wd, cp, tp):
    anym = pl.BlockSpec(memory_space=pl.ANY)
    vm = pl.BlockSpec(memory_space=pltpu.VMEM)
    dma = pltpu.SemaphoreType.DMA
    n = cp * tp
    cap = 2 * gates.shape[1] * h.shape[0] // n
    blocks = pltpu.VMEM((n, cap, h.shape[1]), jnp.bfloat16)
    return pl.pallas_call(
        functools.partial(experts_kernel, cp, tp),
        out_shape=jax.ShapeDtypeStruct(h.shape, jnp.bfloat16),
        in_specs=[anym, anym, anym, vm, anym, anym, anym],
        out_specs=vm,
        scratch_shapes=[
            blocks, blocks, blocks, blocks,
            pltpu.VMEM(wg.shape, jnp.bfloat16), pltpu.VMEM(wu.shape, jnp.bfloat16), pltpu.VMEM(wd.shape, jnp.bfloat16),
            pltpu.VMEM(turned.shape, jnp.float32), pltpu.VMEM(place.shape, jnp.float32), pltpu.VMEM((8, h.shape[0]), jnp.float32),
            pltpu.VMEM(h.shape, jnp.float32),
            dma((n,)), dma((n,)), dma((n,)), dma((n,)), dma((6,)), dma((2,)),
        ],
        compiler_params=pltpu.CompilerParams(collective_id=2, has_side_effects=True, vmem_limit_bytes=62 << 20),
        name='experts',
    )(turned, place, gates.T, h, wg, wu, wd)


def solution(mesh):
    cp = mesh.shape['cp']
    tp = mesh.shape['tp']
    rows_spec = P(('dp', 'cp', 'tp'), None)
    exp_spec = P(('cp', 'tp'), None, None)

    def local(x, idx, gates, wq, wk, wv, wo, w1g, w1u, w2):
        qkv, place, turned = project_exchange(x, idx, wq, wk, wv, cp, tp)
        h = attend(qkv, wo, x, cp, tp)
        return experts(place, turned, gates, h, w1g[0], w1u[0], w2[0], cp, tp)

    return jax.shard_map(local, mesh=mesh, in_specs=(rows_spec, rows_spec, rows_spec, P(None, 'tp'), P(None, 'tp'), P(None, 'tp'), P('tp', None), exp_spec, exp_spec, exp_spec), out_specs=rows_spec, check_vma=False)
```

time: 244 us -> 234 us (0.959); the launches traced: 240 us -> 233 us
  matrix products: 10.7 us -> 0 us
  Pallas kernels: 228 us -> 231 us
    dot_general x4 -> x0, matrix products: 10.7 us -> none  [the longest x1 4.42 us: local(): jnp.dot(pick, h, preferred_element_type=jnp.float32).astype(jnp.bfloat16)]
    pallas_call x1, Pallas kernels: 108 us -> 111 us  [experts(): pl.pallas_call(functools.partial(experts_kernel, cp, tp), out_shape=jax.S...]
where the time goes in v4:
time: 234 us; the launch traced here: 233 us
  Pallas kernels  231 us (99%)
    pallas_call x1, Pallas kernels, experts(): pl.pallas_call(functools.partial(experts_kernel, cp, tp), out_shape=jax.S...  111 us
    pallas_call x1, Pallas kernels, attend(): pl.pallas_call(functools.partial(attend_kernel, cp, tp), out_shape=jax.Sh...  63.4 us
    pallas_call x1, Pallas kernels, project_exchange(): pl.pallas_call(functools.partial(project_kernel, cp, tp), out_shape=(jax....  56.7 us

profile of v4, /device:TPU:103, one launch (start us, length us, event | category | flops | bytes accessed | tf_op | source)
XLA Modules:
  0.0 233.5 jit_solution(861919295584605253)
XLA Ops:
  0.0 56.7 %project_exchange.1 = (bf16[8192,384]{1,0:T(8,128)(2,1)}, f32[256,128]{1,0:T(8,128)}, f32[8,256]{1,0:T(8,128)}) custom-call(bf16[256,2048]{1,0:T(8,128)(2,1)} %x_hbm.3, s32[2,256]{1,0:T(2,128)} %bitcast.8, bf16[2048,256]{1,0:T(8,128)(2,1)} %wq_hbm.1, bf16[2048,256]{1,0:T(8,128)(2,1)} %wk_hbm.1, bf16[2048,256]{1,0:T(8,128)(2,1)} %wv_hbm.1), custom_call_target="tpu_custom_call" | custom-call | tf_op jit(solution)/shard_map/project_exchange/pallas_call | solution.py:298
  56.7 63.4 %attend.1.h_ref = bf16[256,2048]{1,0:T(8,128)(2,1)} custom-call(bf16[8192,384]{1,0:T(8,128)(2,1)} %get-tuple-element.10.qkv_hbm, bf16[256,2048]{1,0:T(8,128)(2,1)} %wo_hbm.1, bf16[256,2048]{1,0:T(8,128)(2,1)} %x_hbm.3), custom_call_target="tpu_custom_call" | custom-call | tf_op jit(solution)/shard_map/attend/pallas_call | solution.py:485
  120.1 111.1 %experts.1 = bf16[256,2048]{1,0:T(8,128)(2,1)} custom-call(f32[8,256]{1,0:T(8,128)} %get-tuple-element.8.turned_hbm, f32[256,128]{1,0:T(8,128)} %get-tuple-element.9.place_hbm, f32[2,256]{1,0:T(2,128)} %bitcast.9, bf16[256,2048]{1,0:T(8,128)(2,1)} %attend.1.h_ref, bf16[2048,1408]{1,0:T(8,128)(2,1)} %bitcast.5, bf16[2048,1408]{1,0:T(8,128)(2,1)} %bitcast.6, ...), custom_call_target="tpu_custom_call" | custom-call | tf_op jit(solution)/shard_map/experts/pallas_call | solution.py:629
  231.1 2.3 copy.12

commit v5 on v4

--- a/solution.py
+++ b/solution.py
@@ -35,16 +35,15 @@
     return lax.rem(c - s * o[0] + cp, cp), 2 * lax.rem(X - s * o[1] + nx, nx) + j
 
 
+def meet(peers):
+    sem = pltpu.get_barrier_semaphore()
+    for pc, pt in peers:
+        pl.semaphore_signal(sem, inc=1, device_id={'cp': pc, 'tp': pt}, device_id_type=MESH)
+    pl.semaphore_wait(sem, len(peers))
+
+
 def greet(cp, tp, c, t):
-    sem = pltpu.get_barrier_semaphore()
-    n = 0
-    for dc in range(cp):
-        for dt in range(tp):
-            if dc or dt:
-                peer = {'cp': lax.rem(c + dc, cp), 'tp': lax.rem(t + dt, tp)}
-                pl.semaphore_signal(sem, inc=1, device_id=peer, device_id_type=MESH)
-                n += 1
-    pl.semaphore_wait(sem, n)
+    meet([(lax.rem(c + dc, cp), lax.rem(t + dt, tp)) for dc in range(cp) for dt in range(tp) if dc or dt])
 
 
 class Gather:
@@ -140,7 +139,8 @@
         ((x_hbm, xs.at[t]), (wq_hbm, wq_ref), (wk_hbm, wk_ref), (wv_hbm, wv_ref), (idx_hbm, idx_ref.at[0:2])))]
     for load in loads:
         load.start()
-    greet(cp, tp, c, t)
+    meet([(c, lax.rem(t + 2, tp)), (c, lax.rem(t + tp - 2, tp)), (c, 2 * X + 1 - i)]
+         + [(lax.rem(c + d, cp), t) for d in range(1, cp)])
 
     np = x_hbm.shape[0] // PIECE
     total = tp * np

time: 234 us -> 232 us (level); the launches traced: 233 us -> 228 us
  Pallas kernels: 231 us -> 226 us
    pallas_call x1, Pallas kernels: 111 us -> 108 us  [experts(): pl.pallas_call(functools.partial(experts_kernel, cp, tp), out_shape=jax.S...]
where the time goes in v5:
time: 232 us; the launch traced here: 228 us
  Pallas kernels  226 us (97%)
    pallas_call x1, Pallas kernels, experts(): pl.pallas_call(functools.partial(experts_kernel, cp, tp), out_shape=jax.S...  108 us
    pallas_call x1, Pallas kernels, attend(): pl.pallas_call(functools.partial(attend_kernel, cp, tp), out_shape=jax.Sh...  62.3 us
    pallas_call x1, Pallas kernels, project_exchange(): pl.pallas_call(functools.partial(project_kernel, cp, tp), out_shape=(jax....  55.3 us

profile of v5, /device:TPU:103, one launch (start us, length us, event | category | flops | bytes accessed | tf_op | source)
XLA Modules:
  0.0 228.0 jit_solution(4191166887423844748)
XLA Ops:
  0.0 55.3 %project_exchange.1 = (bf16[8192,384]{1,0:T(8,128)(2,1)}, f32[256,128]{1,0:T(8,128)}, f32[8,256]{1,0:T(8,128)}) custom-call(bf16[256,2048]{1,0:T(8,128)(2,1)} %x_hbm.3, s32[2,256]{1,0:T(2,128)} %bitcast.8, bf16[2048,256]{1,0:T(8,128)(2,1)} %wq_hbm.1, bf16[2048,256]{1,0:T(8,128)(2,1)} %wk_hbm.1, bf16[2048,256]{1,0:T(8,128)(2,1)} %wv_hbm.1), custom_call_target="tpu_custom_call" | custom-call | tf_op jit(solution)/shard_map/project_exchange/pallas_call | solution.py:298
  55.3 62.3 %attend.1.h_ref = bf16[256,2048]{1,0:T(8,128)(2,1)} custom-call(bf16[8192,384]{1,0:T(8,128)(2,1)} %get-tuple-element.10.qkv_hbm, bf16[256,2048]{1,0:T(8,128)(2,1)} %wo_hbm.1, bf16[256,2048]{1,0:T(8,128)(2,1)} %x_hbm.3), custom_call_target="tpu_custom_call" | custom-call | tf_op jit(solution)/shard_map/attend/pallas_call | solution.py:485
  117.6 108.0 %experts.1 = bf16[256,2048]{1,0:T(8,128)(2,1)} custom-call(f32[8,256]{1,0:T(8,128)} %get-tuple-element.8.turned_hbm, f32[256,128]{1,0:T(8,128)} %get-tuple-element.9.place_hbm, f32[2,256]{1,0:T(2,128)} %bitcast.9, bf16[256,2048]{1,0:T(8,128)(2,1)} %attend.1.h_ref, bf16[2048,1408]{1,0:T(8,128)(2,1)} %bitcast.5, bf16[2048,1408]{1,0:T(8,128)(2,1)} %bitcast.6, ...), custom_call_target="tpu_custom_call" | custom-call | tf_op jit(solution)/shard_map/experts/pallas_call | solution.py:629
  225.7 2.3 %copy.12 = bf16[256,2048]{1,0:T(8,128)(2,1)} copy(bf16[256,2048]{1,0:T(8,128)(2,1)} %experts.1) | data formatting | bytes 2097152
